TPU v7x, 16 devices: a 4x2x1 block of a 4x4x8 slice. The times are simulated.
16 devices in a mesh: dp: 2 (over y, z), tp: 8 (over x, core).
Axes of the slice: x: 4, y: 2, z: 1, core: 2. Of those that a mesh axis runs over, the one named last changes fastest.
The devices are a block of a 4x4x8 slice.
Arguments:
- x_steps: bfloat16 [4, 1024, 512], P(None, 'dp'), parts along dimension 1
- conv_state: bfloat16 [1024, 1024, 3], P('dp', 'tp'), parts along dimension 0
- ssm_state: float32 [1024, 1024, 16], P('dp', 'tp'), parts along dimension 0
- expert_ids: int32 [4, 1024, 1], P(None, 'dp'), parts along dimension 1
- g_in: bfloat16 [512], replicated
- w_in: bfloat16 [512, 2, 1024], P(None, None, 'tp')
- conv_w: bfloat16 [1024, 4], P('tp')
- conv_b: bfloat16 [1024], P('tp')
- w_xp: bfloat16 [1024, 64], P('tp')
- g_dt: bfloat16 [32], replicated
- g_b: bfloat16 [16], replicated
- g_c: bfloat16 [16], replicated
- w_dt: bfloat16 [32, 1024], P(None, 'tp')
- b_dt: bfloat16 [1024], P('tp')
- a_log: float32 [1024, 16], P('tp')
- d_skip: float32 [1024], P('tp')
- w_out: bfloat16 [1024, 512], P('tp')
- g_ff: bfloat16 [512], replicated
- w_router: bfloat16 [512, 16], replicated
- w_gate: bfloat16 [16, 512, 2048], P(None, None, 'tp')
- w_up: bfloat16 [16, 512, 2048], P(None, None, 'tp')
- w_down: bfloat16 [16, 2048, 512], P(None, 'tp')
Outputs:
- output 1: bfloat16 [4, 1024, 512], P(None, 'dp'), parts along dimension 1
- output 2: bfloat16 [1024, 1024, 3], P('dp', 'tp'), parts along dimension 0
- output 3: float32 [1024, 1024, 16], P('dp', 'tp'), parts along dimension 0
There are 2 independent parts. A program takes and returns all parts, laid end to end along the dimension named above; an argument that names none is the same for every part.
All inputs are finite; a program needn't handle non-finite values.
Results may differ from a plain program's by a relative error of at most 0.0159064.
Values are sent between devices in bfloat16 or wider.
A program may use at most 768 MiB of HBM per device.

v0:
```python
import jax
import jax.numpy as jnp
from jax import lax
from jax.sharding import PartitionSpec as P

EPSILON = 1e-6


def rms_norm(tensor_in, gain_vec):
    in_f32 = tensor_in.astype(jnp.float32)
    return in_f32 * lax.rsqrt(jnp.mean(in_f32 * in_f32, axis=-1, keepdims=True) + EPSILON) * gain_vec.astype(jnp.float32)


def solution(mesh):
    act_spec = P(None, "dp", None)
    state_spec = P("dp", "tp", None)
    in_specs = (act_spec, state_spec, state_spec, act_spec, P(None), P(None, None, "tp"), P("tp", None), P("tp"), P("tp", None), P(None), P(None), P(None), P(None, "tp"), P("tp"), P("tp", None), P("tp"), P("tp", None), P(None), P(None, None), P(None, None, "tp"), P(None, None, "tp"), P(None, "tp", None))
    out_specs = (act_spec, state_spec, state_spec)

    def layer_steps(x_steps, conv_state, ssm_state, expert_ids, g_in, w_in, conv_w, conv_b, w_xp, g_dt, g_b, g_c, w_dt, b_dt, a_log, d_skip, w_out, g_ff, w_router, w_gate, w_up, w_down):
        num_steps, batch_loc, d_model = x_steps.shape
        inner_loc = w_in.shape[2]
        dt_rank = w_dt.shape[0]
        state_dim = a_log.shape[1]
        experts = w_gate.shape[0]
        top_k = expert_ids.shape[2]
        route_rows = batch_loc * top_k
        w_in_flat = w_in.reshape(d_model, 2 * inner_loc)
        a_mat = -jnp.exp(a_log)
        conv_wf = conv_w.astype(jnp.float32)
        conv_bf = conv_b.astype(jnp.float32)
        dt_bias = b_dt.astype(jnp.float32)
        conv_st = conv_state
        ssm_st = ssm_state
        step_outs = []
        for step_idx in range(num_steps):
            x_now = x_steps[step_idx]
            ids_now = expert_ids[step_idx]
            norm_in = rms_norm(x_now, g_in).astype(jnp.bfloat16)
            proj_xz = jnp.dot(norm_in, w_in_flat, preferred_element_type=jnp.float32).astype(jnp.bfloat16).reshape(batch_loc, 2, inner_loc)
            x_inner = proj_xz[:, 0]
            z_gate = proj_xz[:, 1]
            conv_win = jnp.concatenate([conv_st, x_inner[:, :, None]], axis=2)
            x_conv = jax.nn.silu(jnp.sum(conv_win.astype(jnp.float32) * conv_wf[None], axis=2) + conv_bf[None]).astype(jnp.bfloat16)
            conv_st = conv_win[:, :, 1:]
            proj_sum = lax.psum(jnp.dot(x_conv, w_xp, preferred_element_type=jnp.float32), "tp")
            dt_low = rms_norm(proj_sum[:, :dt_rank], g_dt)
            b_vec = rms_norm(proj_sum[:, dt_rank:dt_rank + state_dim], g_b)
            c_vec = rms_norm(proj_sum[:, dt_rank + state_dim:], g_c)
            delta_t = jax.nn.softplus(jnp.dot(dt_low.astype(jnp.bfloat16), w_dt, preferred_element_type=jnp.float32) + dt_bias[None])
            xc_f32 = x_conv.astype(jnp.float32)
            ssm_st = jnp.exp(delta_t[:, :, None] * a_mat[None]) * ssm_st + (delta_t * xc_f32)[:, :, None] * b_vec[:, None, :]
            y_gated = ((jnp.sum(ssm_st * c_vec[:, None, :], axis=2) + d_skip[None] * xc_f32) * jax.nn.silu(z_gate.astype(jnp.float32))).astype(jnp.bfloat16)
            mix_sum = lax.psum(jnp.dot(y_gated, w_out, preferred_element_type=jnp.float32).astype(jnp.bfloat16), "tp")
            resid_mid = (x_now.astype(jnp.float32) + mix_sum.astype(jnp.float32)).astype(jnp.bfloat16)
            moe_in = rms_norm(resid_mid, g_ff).astype(jnp.bfloat16)
            route_prob = jax.nn.softmax(jnp.dot(moe_in, w_router, preferred_element_type=jnp.float32), axis=-1)
            flat_ids = ids_now.reshape(route_rows)
            sort_order = jnp.argsort(flat_ids, stable=True)
            tok_rows = sort_order // top_k
            counts = jnp.bincount(flat_ids, length=experts).astype(jnp.int32)
            x_rows = jnp.take(moe_in, tok_rows, axis=0)
            gate_h = lax.ragged_dot(x_rows, w_gate, counts, preferred_element_type=jnp.float32)
            up_h = lax.ragged_dot(x_rows, w_up, counts, preferred_element_type=jnp.float32)
            hidden = (jax.nn.silu(gate_h) * up_h).astype(jnp.bfloat16)
            y_rows = lax.ragged_dot(hidden, w_down, counts, preferred_element_type=jnp.float32)
            gate_rows = jnp.take(jnp.take_along_axis(route_prob, ids_now, axis=1).reshape(route_rows), sort_order)
            moe_part = jax.ops.segment_sum(y_rows * gate_rows[:, None], tok_rows, num_segments=batch_loc)
            moe_sum = lax.psum(moe_part.astype(jnp.bfloat16), "tp")
            step_outs.append((resid_mid.astype(jnp.float32) + moe_sum.astype(jnp.float32)).astype(jnp.bfloat16))
        return jnp.stack(step_outs), conv_st, ssm_st

    return jax.shard_map(layer_steps, mesh=mesh, in_specs=in_specs, out_specs=out_specs, check_vma=False)
```

profile of v0, /device:TPU:112, one launch (start us, length us, event | category | flops | bytes accessed | tf_op | source)
XLA Modules:
  0.0 450.1 jit_solution(17620508475730393148)
XLA Ops:
  10.0 2.0 fusion.16
  12.0 1.6 convolution_convert_fusion.6
  15.6 1.4 convolution_convert_fusion.7
  17.8 1.4 convolution_convert_fusion.5
  28.5 3.8 sort.59
  32.2 3.8 sort.60
  36.6 3.8 sort.62
  45.3 1.7 copy.53
  46.9 1.7 copy.55
  48.6 1.6 copy.52
  50.3 1.7 copy.54
  52.6 29.4 %all-reduce.7.cloned.1.call-done = (f32[512,64]{0,1:T(8,128)}, f32[512,64]{0,1:T(8,128)}, f32[512,64]{0,1:T(8,128)}, f32[512,64]{0,1:T(8,128)}) async-done(((f32[512,64]{0,1:T(8,128)}, f32[512,64]{0,1:T(8,128)}, f32[512,64]{0,1:T(8,128)}, f32[512,64]{0,1:T(8,128)}), (f32[512,64]{0,1:T(8,128)}, f32[512,64]{0,1:T(8,128)}, f32[512,64]{0,1:T(8,128)}, f32[512,64]{0,1:T(8,128)})) %all-reduce.7.cloned.1.call-update) | async-done | bytes 524304 | tf_op jit(solution)/shard_map/psum | solution.py:46
  91.1 1.6 multiply_multiply_fusion.5
  94.0 1.6 copy.49
  95.6 1.6 copy.48
  97.2 1.6 copy.45
  98.8 1.6 copy.44
  101.8 1.4 convert_multiply_fusion.17
  106.0 13.4 %multiply_reduce_fusion = (f32[512,128]{1,0:T(8,128)S(1)}, f32[512,128,16]{1,2,0:T(8,128)}, f32[512,128]{1,0:T(8,128)S(1)}, f32[512,128]{1,0:T(8,128)S(1)}, f32[512,128]{1,0:T(8,128)S(1)}) fusion(f32[512,16]{1,0:T(8,128)} %copy.49, f32[512,16]{1,0:T(8,128)} %copy.48, f32[512,128]{1,0:T(8,128)S(1)} %get-tuple-element.164, f32[512,16]{1,0:T(8,128)} %copy.44, ...), kind=kLoop, calls=%fused_computation.20 | loop fusion | flops 24903680 | bytes 11804672 | tf_op jit(solution)/shard_map/reduce_sum | solution.py:53
  124.1 4.8 %scatter_custom_fusion = s32[16]{0:T(128)} fusion(s32[512]{0:T(512)} %bitcast.242, s32[512]{0:T(512)S(1)} %broadcast.454, s32[]{:T(128)} %constant.124.clone.1), kind=kCustom, calls=%fused_computation.363 | custom fusion | flops 512 | bytes 576 | tf_op jit(solution)/shard_map/scatter-add | solution.py:61
  128.9 4.8 %scatter_custom_fusion.2 = s32[16]{0:T(128)} fusion(s32[512]{0:T(512)} %bitcast.241, s32[512]{0:T(512)S(1)} %broadcast.454, s32[]{:T(128)} %constant.124.clone.1), kind=kCustom, calls=%fused_computation.361 | custom fusion | flops 512 | bytes 576 | tf_op jit(solution)/shard_map/scatter-add | solution.py:61
  133.8 4.8 %scatter_custom_fusion.4 = s32[16]{0:T(128)} fusion(s32[512]{0:T(512)} %bitcast.240, s32[512]{0:T(512)S(1)} %broadcast.454, s32[]{:T(128)} %constant.124.clone.1), kind=kCustom, calls=%fused_computation.359 | custom fusion | flops 512 | bytes 576 | tf_op jit(solution)/shard_map/scatter-add | solution.py:61
  138.5 4.7 %scatter_custom_fusion.6 = s32[16]{0:T(128)} fusion(s32[512]{0:T(512)} %bitcast.239, s32[512]{0:T(512)S(1)} %broadcast.454, s32[]{:T(128)} %constant.124.clone.1), kind=kCustom, calls=%fused_computation.357 | custom fusion | flops 512 | bytes 576 | tf_op jit(solution)/shard_map/scatter-add | solution.py:61
  143.3 1.8 ragged-dot-metadata
  145.0 1.8 ragged-dot-metadata.1
  146.8 1.8 ragged-dot-metadata.2
  148.6 1.8 ragged-dot-metadata.3
  150.4 3.8 sort.61
  154.4 26.6 %all-reduce.11.cloned.1.call-done = (bf16[512,512]{1,0:T(8,128)(2,1)}, bf16[512,512]{1,0:T(8,128)(2,1)}, bf16[512,512]{1,0:T(8,128)(2,1)}, bf16[512,512]{1,0:T(8,128)(2,1)}) async-done(((bf16[512,512]{1,0:T(8,128)(2,1)}, bf16[512,512]{1,0:T(8,128)(2,1)}, bf16[512,512]{1,0:T(8,128)(2,1)}, bf16[512,512]{1,0:T(8,128)(2,1)}), (bf16[512,512]{1,0:T(8,128)(2,1)}, bf16[512,512]{1,0:T(8,128)(2,1)}, ...) | async-done | bytes 2097168 | tf_op jit(solution)/shard_map/psum | solution.py:54
  180.9 2.4 fusion.24
  185.4 2.6 gather_fusion.6
  188.4 2.0 gather_fusion.9
  190.4 4.5 %gather_fusion.1 = f32[512]{0:T(512)S(1)} fusion(f32[512,16]{0,1:T(8,128)S(1)} %fusion.140, s32[512]{0:T(512)S(1)} %bitcast.224), kind=kCustom, calls=%fused_computation.1.clone | custom fusion | bytes 8192 | tf_op jit(solution)/shard_map/jit(take_along_axis)/gather | solution.py:67
  195.0 4.5 %gather_fusion.4 = f32[512]{0:T(512)S(1)} fusion(f32[512,16]{0,1:T(8,128)S(1)} %fusion.142, s32[512]{0:T(512)S(1)} %bitcast.222), kind=kCustom, calls=%fused_computation.6.clone | custom fusion | bytes 8192 | tf_op jit(solution)/shard_map/jit(take_along_axis)/gather | solution.py:67
  199.5 4.5 %gather_fusion.7 = f32[512]{0:T(512)S(1)} fusion(f32[512,16]{0,1:T(8,128)S(1)} %fusion.144, s32[512]{0:T(512)S(1)} %bitcast.223), kind=kCustom, calls=%fused_computation.7.clone | custom fusion | bytes 8192 | tf_op jit(solution)/shard_map/jit(take_along_axis)/gather | solution.py:67
  204.1 4.5 %gather_fusion.10 = f32[512]{0:T(512)S(1)} fusion(f32[512,16]{0,1:T(8,128)S(1)} %fusion.146, s32[512]{0:T(512)S(1)} %bitcast.221), kind=kCustom, calls=%fused_computation.8.clone | custom fusion | bytes 8192 | tf_op jit(solution)/shard_map/jit(take_along_axis)/gather | solution.py:67
  208.7 3.5 gather_fusion.11
  212.2 3.5 gather_fusion.8
  216.7 8.8 %ragged-dot-none.1 = f32[512,256]{1,0:T(8,128)} custom-call(s32[1]{0:T(128)} %get-tuple-element.14, s32[17]{0:T(128)} %get-tuple-element.15, s32[17]{0:T(128)} %get-tuple-element.16, s32[17]{0:T(128)} %get-tuple-element.17, s32[1]{0:T(128)} %get-tuple-element.14, bf16[512,512]{1,0:T(8,128)(2,1)} %broadcast_select_fusion, bf16[16,512,256]{2,1,0:T(8,128)(2,1)} %param.48), custom_call_target="tpu_custom_call" | custom-call | flops 134217728 | bytes 5242944 | tf_op jit(solution)/shard_map/ragged_dot_general/ragged-dot-none
  225.5 8.8 %ragged-dot-none.2 = f32[512,256]{1,0:T(8,128)} custom-call(s32[1]{0:T(128)} %get-tuple-element.14, s32[17]{0:T(128)} %get-tuple-element.15, s32[17]{0:T(128)} %get-tuple-element.16, s32[17]{0:T(128)} %get-tuple-element.17, s32[1]{0:T(128)} %get-tuple-element.14, bf16[512,512]{1,0:T(8,128)(2,1)} %broadcast_select_fusion, bf16[16,512,256]{2,1,0:T(8,128)(2,1)} %param.47), custom_call_target="tpu_custom_call" | custom-call | flops 134217728 | bytes 5242944 | tf_op jit(solution)/shard_map/ragged_dot_general/ragged-dot-none
  235.2 9.1 %ragged-dot-none.4 = f32[512,256]{1,0:T(8,128)} custom-call(s32[1]{0:T(128)} %get-tuple-element.26, s32[17]{0:T(128)} %get-tuple-element.27, s32[17]{0:T(128)} %get-tuple-element.28, s32[17]{0:T(128)} %get-tuple-element.29, s32[1]{0:T(128)} %get-tuple-element.26, bf16[512,512]{1,0:T(8,128)(2,1)} %broadcast_select_fusion.1, bf16[16,512,256]{2,1,0:T(8,128)(2,1)} %param.48), custom_call_target="tpu_custom_call" | custom-call | flops 134217728 | bytes 5242944 | tf_op jit(solution)/shard_map/ragged_dot_general/ragged-dot-none
  244.3 9.1 %ragged-dot-none.5 = f32[512,256]{1,0:T(8,128)} custom-call(s32[1]{0:T(128)} %get-tuple-element.26, s32[17]{0:T(128)} %get-tuple-element.27, s32[17]{0:T(128)} %get-tuple-element.28, s32[17]{0:T(128)} %get-tuple-element.29, s32[1]{0:T(128)} %get-tuple-element.26, bf16[512,512]{1,0:T(8,128)(2,1)} %broadcast_select_fusion.1, bf16[16,512,256]{2,1,0:T(8,128)(2,1)} %param.47), custom_call_target="tpu_custom_call" | custom-call | flops 134217728 | bytes 5242944 | tf_op jit(solution)/shard_map/ragged_dot_general/ragged-dot-none
  253.5 2.0 gather_fusion
  255.5 3.5 gather_fusion.2
  259.9 13.9 %ragged-dot-none.10 = f32[512,256]{1,0:T(8,128)} custom-call(s32[1]{0:T(128)} %get-tuple-element.50, s32[17]{0:T(128)} %get-tuple-element.51, s32[17]{0:T(128)} %get-tuple-element.52, s32[17]{0:T(128)} %get-tuple-element.53, s32[1]{0:T(128)} %get-tuple-element.50, bf16[512,512]{1,0:T(8,128)(2,1)} %broadcast_select_fusion.3, bf16[16,512,256]{2,1,0:T(8,128)(2,1)} %param.48), custom_call_target="tpu_custom_call" | custom-call | flops 134217728 | bytes 5242944 | tf_op jit(solution)/shard_map/ragged_dot_general/ragged-dot-none
  273.8 13.6 %ragged-dot-none.11 = f32[512,256]{1,0:T(8,128)} custom-call(s32[1]{0:T(128)} %get-tuple-element.50, s32[17]{0:T(128)} %get-tuple-element.51, s32[17]{0:T(128)} %get-tuple-element.52, s32[17]{0:T(128)} %get-tuple-element.53, s32[1]{0:T(128)} %get-tuple-element.50, bf16[512,512]{1,0:T(8,128)(2,1)} %broadcast_select_fusion.3, bf16[16,512,256]{2,1,0:T(8,128)(2,1)} %param.47), custom_call_target="tpu_custom_call" | custom-call | flops 134217728 | bytes 5242944 | tf_op jit(solution)/shard_map/ragged_dot_general/ragged-dot-none
  287.4 2.0 gather_fusion.3
  289.4 3.5 gather_fusion.5
  293.9 9.1 %ragged-dot-none.7 = f32[512,256]{1,0:T(8,128)} custom-call(s32[1]{0:T(128)} %get-tuple-element.38, s32[17]{0:T(128)} %get-tuple-element.39, s32[17]{0:T(128)} %get-tuple-element.40, s32[17]{0:T(128)} %get-tuple-element.41, s32[1]{0:T(128)} %get-tuple-element.38, bf16[512,512]{1,0:T(8,128)(2,1)} %broadcast_select_fusion.2, bf16[16,512,256]{2,1,0:T(8,128)(2,1)} %param.48), custom_call_target="tpu_custom_call" | custom-call | flops 134217728 | bytes 5242944 | tf_op jit(solution)/shard_map/ragged_dot_general/ragged-dot-none
  302.9 9.1 %ragged-dot-none.8 = f32[512,256]{1,0:T(8,128)} custom-call(s32[1]{0:T(128)} %get-tuple-element.38, s32[17]{0:T(128)} %get-tuple-element.39, s32[17]{0:T(128)} %get-tuple-element.40, s32[17]{0:T(128)} %get-tuple-element.41, s32[1]{0:T(128)} %get-tuple-element.38, bf16[512,512]{1,0:T(8,128)(2,1)} %broadcast_select_fusion.2, bf16[16,512,256]{2,1,0:T(8,128)(2,1)} %param.47), custom_call_target="tpu_custom_call" | custom-call | flops 134217728 | bytes 5242944 | tf_op jit(solution)/shard_map/ragged_dot_general/ragged-dot-none
  312.0 1.9 multiply_convert_fusion.2
  313.9 9.3 %ragged-dot-none.6 = f32[512,512]{1,0:T(8,128)} custom-call(s32[1]{0:T(128)} %get-tuple-element.38, s32[17]{0:T(128)} %get-tuple-element.39, s32[17]{0:T(128)} %get-tuple-element.40, s32[17]{0:T(128)} %get-tuple-element.41, s32[1]{0:T(128)} %get-tuple-element.38, bf16[512,256]{1,0:T(8,128)(2,1)} %multiply_convert_fusion.2, bf16[16,256,512]{2,1,0:T(8,128)(2,1)} %param.49), custom_call_target="tpu_custom_call" | custom-call | flops 134217728 | bytes 5505088 | tf_op jit(solution)/shard_map/ragged_dot_general/ragged-dot-none
  323.2 4.6 %scatter_custom_fusion.3 = f32[512,512]{1,0:T(8,128)S(1)} fusion(s32[512]{0:T(512)S(1)} %copy-done.40, f32[512,512]{1,0:T(8,128)} %ragged-dot-none.6, f32[512]{0:T(512)S(1)} %get-tuple-element.99, f32[]{:T(128)} %constant.118.clone.1), kind=kCustom, calls=%fused_computation.107 | custom fusion | flops 524288 | bytes 2099204 | tf_op jit(solution)/shard_map/scatter-add | solution.py:68
  329.6 13.9 %ragged-dot-none.9 = f32[512,512]{1,0:T(8,128)} custom-call(s32[1]{0:T(128)} %get-tuple-element.50, s32[17]{0:T(128)} %get-tuple-element.51, s32[17]{0:T(128)} %get-tuple-element.52, s32[17]{0:T(128)} %get-tuple-element.53, s32[1]{0:T(128)} %get-tuple-element.50, bf16[512,256]{1,0:T(8,128)(2,1)} %multiply_convert_fusion.3, bf16[16,256,512]{2,1,0:T(8,128)(2,1)} %param.49), custom_call_target="tpu_custom_call" | custom-call | flops 134217728 | bytes 5505088 | tf_op jit(solution)/shard_map/ragged_dot_general/ragged-dot-none
  343.5 4.6 %scatter_custom_fusion.1 = f32[512,512]{1,0:T(8,128)S(1)} fusion(s32[512]{0:T(512)S(1)} %copy-done.38, f32[512,512]{1,0:T(8,128)} %ragged-dot-none.9, f32[512]{0:T(512)S(1)} %get-tuple-element.97, f32[]{:T(128)} %constant.118.clone.1), kind=kCustom, calls=%fused_computation.110 | custom fusion | flops 524288 | bytes 2099204 | tf_op jit(solution)/shard_map/scatter-add | solution.py:68
  349.9 9.6 %ragged-dot-none.3 = f32[512,512]{1,0:T(8,128)} custom-call(s32[1]{0:T(128)} %get-tuple-element.26, s32[17]{0:T(128)} %get-tuple-element.27, s32[17]{0:T(128)} %get-tuple-element.28, s32[17]{0:T(128)} %get-tuple-element.29, s32[1]{0:T(128)} %get-tuple-element.26, bf16[512,256]{1,0:T(8,128)(2,1)} %multiply_convert_fusion.1, bf16[16,256,512]{2,1,0:T(8,128)(2,1)} %param.49), custom_call_target="tpu_custom_call" | custom-call | flops 134217728 | bytes 5505088 | tf_op jit(solution)/shard_map/ragged_dot_general/ragged-dot-none
  359.5 4.6 %scatter_custom_fusion.5 = f32[512,512]{1,0:T(8,128)S(1)} fusion(s32[512]{0:T(512)S(1)} %get-tuple-element.12, f32[512,512]{1,0:T(8,128)} %ragged-dot-none.3, f32[512]{0:T(512)S(1)} %get-tuple-element.101, f32[]{:T(128)} %constant.118.clone.1), kind=kCustom, calls=%fused_computation.104 | custom fusion | flops 524288 | bytes 2099204 | tf_op jit(solution)/shard_map/scatter-add | solution.py:68
  365.9 8.9 %ragged-dot-none = f32[512,512]{1,0:T(8,128)} custom-call(s32[1]{0:T(128)} %get-tuple-element.14, s32[17]{0:T(128)} %get-tuple-element.15, s32[17]{0:T(128)} %get-tuple-element.16, s32[17]{0:T(128)} %get-tuple-element.17, s32[1]{0:T(128)} %get-tuple-element.14, bf16[512,256]{1,0:T(8,128)(2,1)} %multiply_convert_fusion, bf16[16,256,512]{2,1,0:T(8,128)(2,1)} %param.49), custom_call_target="tpu_custom_call" | custom-call | flops 134217728 | bytes 5505088 | tf_op jit(solution)/shard_map/ragged_dot_general/ragged-dot-none
  374.8 5.5 %scatter_custom_fusion.7 = f32[512,512]{1,0:T(8,128)} fusion(s32[512]{0:T(512)S(1)} %copy-done.36, f32[512,512]{1,0:T(8,128)} %ragged-dot-none, f32[512]{0:T(512)S(1)} %get-tuple-element.103, f32[]{:T(128)} %constant.118.clone.1), kind=kCustom, calls=%fused_computation.101 | custom fusion | flops 524288 | bytes 2099204 | tf_op jit(solution)/shard_map/scatter-add | solution.py:68
  380.3 2.1 convert_element_type.404
  382.5 1.7 fusion.80
  384.2 54.6 %all-reduce.9.cloned.1.call-done = (bf16[512,512]{1,0:T(8,128)(2,1)}, bf16[512,512]{1,0:T(8,128)(2,1)}, bf16[512,512]{1,0:T(8,128)(2,1)}, bf16[512,512]{1,0:T(8,128)(2,1)}) async-done(((bf16[512,512]{1,0:T(8,128)(2,1)}, bf16[512,512]{1,0:T(8,128)(2,1)}, bf16[512,512]{1,0:T(8,128)(2,1)}, bf16[512,512]{1,0:T(8,128)(2,1)}), (bf16[512,512]{1,0:T(8,128)(2,1)}, bf16[512,512]{1,0:T(8,128)(2,1)}, ...) | async-done | bytes 2097168 | tf_op jit(solution)/shard_map/psum | solution.py:69
  438.8 2.7 fusion.51
  441.5 1.6 pad_maximum_fusion
  (219 shorter events, 51.4 us)
Async XLA Ops:
  7.2 112.2 %copy-start = (bf16[128,512]{1,0:T(8,128)(2,1)S(1)}, bf16[128,512]{1,0:T(8,128)(2,1)}, u32[]{:S(2)}) copy-start(bf16[128,512]{1,0:T(8,128)(2,1)} %param.44) | copy-start | bytes 393220
  7.2 7.2 %copy-start.2 = (bf16[4,512,512]{2,1,0:T(8,128)(2,1)S(1)}, bf16[4,512,512]{2,1,0:T(8,128)(2,1)}, u32[]{:S(2)}) copy-start(bf16[4,512,512]{2,1,0:T(8,128)(2,1)} %param.28) | copy-start | bytes 6291460
  7.2 7.2 %copy-start.48 = (bf16[512,2,128]{2,1,0:T(2,128)(2,1)S(1)}, bf16[512,2,128]{2,1,0:T(2,128)(2,1)}, u32[]{:S(2)}) copy-start(bf16[512,2,128]{2,1,0:T(2,128)(2,1)} %param.33) | copy-start | bytes 786436
  7.2 74.8 %all-reduce.7.cloned.1.call-start = ((), (), s32[]{:S(2)}) async-start(), calls=%async_computation | async-start | bytes 1048576 | tf_op jit(solution)/shard_map/psum | solution.py:46
  13.5 6.5 %copy-start.18 = (bf16[512,128,3]{1,0,2:T(8,128)(2,1)S(1)}, bf16[512,128,3]{1,0,2:T(8,128)(2,1)}, u32[]{:S(2)}) copy-start(bf16[512,128,3]{1,0,2:T(8,128)(2,1)} %param.29) | copy-start | bytes 1179652
  19.2 3.1 copy-start.25
  20.2 0.7 copy-start.9
  22.3 1.7 copy-start.19
  22.3 2.5 copy-start.23
  22.3 2.5 copy-start.21
  25.7 155.2 %all-reduce.11.cloned.1.call-start = ((), (), s32[]{:S(2)}) async-start(), calls=%async_computation.2 | async-start | bytes 4194304 | tf_op jit(solution)/shard_map/psum | solution.py:54
  32.2 4.4 copy-start.37
  36.0 56.7 %copy-start.39 = (s32[512]{0:T(512)}, s32[512]{0:T(512)S(1)}, u32[]{:S(2)}) copy-start(s32[512]{0:T(512)S(1)} %get-tuple-element.11) | copy-start | bytes 6148
  40.4 52.4 %copy-start.35 = (s32[512]{0:T(512)}, s32[512]{0:T(512)S(1)}, u32[]{:S(2)}) copy-start(s32[512]{0:T(512)S(1)} %get-tuple-element.13) | copy-start | bytes 6148
  92.7 11.9 %copy-start.46 = (f32[512]{0:T(512)S(1)}, f32[512]{0:T(512)}, u32[]{:S(2)}) copy-start(f32[512]{0:T(512)} %add_rsqrt_fusion.13) | copy-start | bytes 6148
  92.7 11.9 %copy-start.50 = (f32[32]{0:T(128)S(1)}, f32[32]{0:T(128)}, u32[]{:S(2)}) copy-start(f32[32]{0:T(128)} %convert_element_type.322) | copy-start | bytes 388
  105.9 13.5 %copy-start.24 = (bf16[512,128]{1,0:T(8,128)(2,1)S(1)}, bf16[512,128]{1,0:T(8,128)(2,1)}, u32[]{:S(2)}) copy-start(bf16[512,128]{1,0:T(8,128)(2,1)} %copy-done.23) | copy-start | bytes 393220
  105.9 13.5 %copy-start.30 = (bf16[512,1,128]{2,0,1:T(8,128)(2,1)S(1)}, bf16[512,1,128]{2,0,1:T(8,128)(2,1)}, u32[]{:S(2)}) copy-start(bf16[512,1,128]{2,0,1:T(8,128)(2,1)} %copy.55) | copy-start | bytes 393220
  105.9 13.5 %copy-start.49 = (f32[128]{0:T(128)S(1)}, f32[128]{0:T(128)}, u32[]{:S(2)}) copy-start(f32[128]{0:T(128)} %param.43) | copy-start | bytes 1540
  105.9 14.7 %copy-start.22 = (bf16[512,128]{1,0:T(8,128)(2,1)S(1)}, bf16[512,128]{1,0:T(8,128)(2,1)}, u32[]{:S(2)}) copy-start(bf16[512,128]{1,0:T(8,128)(2,1)} %copy-done.21) | copy-start | bytes 393220
  105.9 14.7 %copy-start.29 = (bf16[512,1,128]{2,0,1:T(8,128)(2,1)S(1)}, bf16[512,1,128]{2,0,1:T(8,128)(2,1)}, u32[]{:S(2)}) copy-start(bf16[512,1,128]{2,0,1:T(8,128)(2,1)} %copy.52) | copy-start | bytes 393220
  105.9 15.8 %copy-start.20 = (bf16[512,128]{1,0:T(8,128)(2,1)S(1)}, bf16[512,128]{1,0:T(8,128)(2,1)}, u32[]{:S(2)}) copy-start(bf16[512,128]{1,0:T(8,128)(2,1)} %copy-done.19) | copy-start | bytes 393220
  105.9 15.8 %copy-start.28 = (bf16[512,1,128]{2,0,1:T(8,128)(2,1)S(1)}, bf16[512,1,128]{2,0,1:T(8,128)(2,1)}, u32[]{:S(2)}) copy-start(bf16[512,1,128]{2,0,1:T(8,128)(2,1)} %copy.54) | copy-start | bytes 393220
  119.3 3.5 copy-start.27
  119.4 4.7 %copy-start.34 = (s32[512]{0:T(512)S(1)}, s32[512]{0:T(512)}, u32[]{:S(2)}) copy-start(s32[512]{0:T(512)} %compare_select_fusion.10) | copy-start | bytes 6148
  119.4 4.7 %copy-start.47 = (bf16[512]{0:T(512)(128)(2,1)S(1)}, bf16[512]{0:T(512)(128)(2,1)}, u32[]{:S(2)}) copy-start(bf16[512]{0:T(512)(128)(2,1)} %param.45) | copy-start | bytes 3076
  119.4 31.0 %copy-start.45 = (s32[1,512,1]{1,2,0:T(1,128)S(1)}, s32[1,512,1]{1,2,0:T(1,128)}, u32[]{:S(2)}) copy-start(s32[1,512,1]{1,2,0:T(1,128)} %get-tuple-element.149) | copy-start | bytes 6148
  119.4 34.8 %copy-start.33 = (s32[512]{0:T(512)S(1)}, s32[512]{0:T(512)}, u32[]{:S(2)}) copy-start(s32[512]{0:T(512)} %compare_select_fusion.8) | copy-start | bytes 6148
  119.4 34.8 %copy-start.41 = (s32[512,1,1]{0,2,1:T(1,128)S(1)}, s32[512,1,1]{0,2,1:T(1,128)}, u32[]{:S(2)}) copy-start(s32[512,1,1]{0,2,1:T(1,128)} %get-tuple-element.138) | copy-start | bytes 6148
  119.4 34.8 %copy-start.42 = (s32[512,1,1]{0,2,1:T(1,128)S(1)}, s32[512,1,1]{0,2,1:T(1,128)}, u32[]{:S(2)}) copy-start(s32[512,1,1]{0,2,1:T(1,128)} %get-tuple-element.141) | copy-start | bytes 6148
  119.5 34.8 %copy-start.43 = (s32[512,1,1]{0,2,1:T(1,128)S(1)}, s32[512,1,1]{0,2,1:T(1,128)}, u32[]{:S(2)}) copy-start(s32[512,1,1]{0,2,1:T(1,128)} %get-tuple-element.143) | copy-start | bytes 6148
  119.5 34.8 %copy-start.44 = (s32[512,1,1]{0,2,1:T(1,128)S(1)}, s32[512,1,1]{0,2,1:T(1,128)}, u32[]{:S(2)}) copy-start(s32[512,1,1]{0,2,1:T(1,128)} %get-tuple-element.145) | copy-start | bytes 6148
  124.0 314.8 %all-reduce.9.cloned.1.call-start = ((), (), s32[]{:S(2)}) async-start(), calls=%async_computation.1 | async-start | bytes 4194304 | tf_op jit(solution)/shard_map/psum | solution.py:69
  180.9 2.5 copy-start.3
  180.9 2.5 copy-start.5
  180.9 2.5 copy-start.6
  180.9 2.6 copy-start.7
  180.9 2.8 copy-start.8
  183.4 1.1 copy-start.26
  190.4 18.3 %copy-start.31 = (s32[4,512,1]{1,2,0:T(1,128)S(1)}, s32[4,512,1]{1,2,0:T(1,128)}, u32[]{:S(2)}) copy-start(s32[4,512,1]{1,2,0:T(1,128)} %param.31) | copy-start | bytes 24580
  199.5 16.2 %copy-start.36 = (s32[512]{0:T(512)S(1)}, s32[512]{0:T(512)}, u32[]{:S(2)}) copy-start(s32[512]{0:T(512)} %copy-done.35) | copy-start | bytes 6148
  216.7 17.6 %copy-start.17 = (bf16[512,512]{1,0:T(8,128)(2,1)S(1)}, bf16[512,512]{1,0:T(8,128)(2,1)}, u32[]{:S(2)}) copy-start(bf16[512,512]{1,0:T(8,128)(2,1)} %gather_fusion.6) | copy-start | bytes 1572868
  235.2 18.3 %copy-start.32 = (s32[1024]{0:T(1024)S(1)}, s32[1024]{0:T(1024)}, u32[]{:S(2)}) copy-start(s32[1024]{0:T(1024)} %pad_clamp_fusion.3) | copy-start | bytes 12292
  253.5 5.5 %copy-start.38 = (s32[512]{0:T(512)S(1)}, s32[512]{0:T(512)}, u32[]{:S(2)}) copy-start(s32[512]{0:T(512)} %copy-done.37) | copy-start | bytes 6148
  287.4 5.5 %copy-start.40 = (s32[512]{0:T(512)S(1)}, s32[512]{0:T(512)}, u32[]{:S(2)}) copy-start(s32[512]{0:T(512)} %copy-done.39) | copy-start | bytes 6148
  302.9 9.1 %copy-start.16 = (f32[512,256]{1,0:T(8,128)S(1)}, f32[512,256]{1,0:T(8,128)}, u32[]{:S(2)}) copy-start(f32[512,256]{1,0:T(8,128)} %ragged-dot-none.7) | copy-start | bytes 1572868
  313.9 14.8 %copy-start.14 = (f32[512,256]{1,0:T(8,128)S(1)}, f32[512,256]{1,0:T(8,128)}, u32[]{:S(2)}) copy-start(f32[512,256]{1,0:T(8,128)} %ragged-dot-none.10) | copy-start | bytes 1572868
  313.9 14.8 %copy-start.15 = (f32[512,256]{1,0:T(8,128)S(1)}, f32[512,256]{1,0:T(8,128)}, u32[]{:S(2)}) copy-start(f32[512,256]{1,0:T(8,128)} %ragged-dot-none.11) | copy-start | bytes 1572868
  329.6 19.4 %copy-start.12 = (f32[512,256]{1,0:T(8,128)S(1)}, f32[512,256]{1,0:T(8,128)}, u32[]{:S(2)}) copy-start(f32[512,256]{1,0:T(8,128)} %ragged-dot-none.4) | copy-start | bytes 1572868
  329.6 19.4 %copy-start.13 = (f32[512,256]{1,0:T(8,128)S(1)}, f32[512,256]{1,0:T(8,128)}, u32[]{:S(2)}) copy-start(f32[512,256]{1,0:T(8,128)} %ragged-dot-none.5) | copy-start | bytes 1572868
  349.9 15.2 %copy-start.10 = (f32[512,256]{1,0:T(8,128)S(1)}, f32[512,256]{1,0:T(8,128)}, u32[]{:S(2)}) copy-start(f32[512,256]{1,0:T(8,128)} %ragged-dot-none.1) | copy-start | bytes 1572868
  349.9 15.2 %copy-start.11 = (f32[512,256]{1,0:T(8,128)S(1)}, f32[512,256]{1,0:T(8,128)}, u32[]{:S(2)}) copy-start(f32[512,256]{1,0:T(8,128)} %ragged-dot-none.2) | copy-start | bytes 1572868
  374.8 64.0 %copy-start.4 = (bf16[4,512,512]{2,1,0:T(8,128)(2,1)S(1)}, bf16[4,512,512]{2,1,0:T(8,128)(2,1)}, u32[]{:S(2)}) copy-start(bf16[4,512,512]{2,1,0:T(8,128)(2,1)} %param.28) | copy-start | bytes 6291460
  438.8 4.3 copy-start.1
Sparse Core Ops, SparseCore 0:
  25.8 56.1 all-reduce.6
  124.1 56.7 all-reduce.10
  361.4 82.1 all-reduce.8
where the time goes:
time: 464 us; the launch traced here: 450 us
  waiting for transfers between devices  137 us (30%)
  other arithmetic  114 us (25%)
  Pallas kernels  109 us (23%)
  local copies, waits for them, and re-layouts  60.6 us (13%)
  matrix products  19 us (4%)
  between operations  15.3 us (3%)
    another operation x12, Pallas kernels  102 us
    psum x1, waiting for transfers between devices, layer_steps(): moe_sum = lax.psum(moe_part.astype(jnp.bfloat16), 'tp')  80.6 us
    psum x1, waiting for transfers between devices, layer_steps(): lax.psum(jnp.dot(x_conv, w_xp, preferred_element_type=jnp.float32), 'tp')  29.4 us
    psum x1, waiting for transfers between devices, layer_steps(): lax.psum(jnp.dot(y_gated, w_out, preferred_element_type=jnp.float32).asty...  26.6 us
    scatter-add x4, other arithmetic, layer_steps(): jax.ops.segment_sum(y_rows * gate_rows[:, None], tok_rows, num_segments=b...  19.4 us
    scatter-add x4, other arithmetic, layer_steps(): counts = jnp.bincount(flat_ids, length=experts).astype(jnp.int32)  19.1 us
    gather x4, local copies, waits for them, and re-layouts, layer_steps(): jnp.take_along_axis(route_prob, ids_now, axis=1).reshape(route_rows)  18.2 us
    sort x4, other arithmetic, layer_steps(): sort_order = jnp.argsort(flat_ids, stable=True)  15.1 us
  transfers between devices with their start and end apart: 3, of which 3 were waited for; matrix products, arithmetic and copies ran while one was open for 11% of the time, Pallas kernels for 2%

commit v1 on v0

v1 whole, which is shorter than its diff:
```python
import functools
import math

import jax
import jax.numpy as jnp
from jax import lax
from jax.experimental import pallas as pl
from jax.experimental.pallas import tpu as pltpu
from jax.sharding import PartitionSpec as P

EPSILON = 1e-6
F32 = jnp.float32
BF16 = jnp.bfloat16
CHUNK_ROWS = 64
GROUP = 4
LOG2E = math.log2(math.e)


class Lazy:
    def __init__(self, **makers):
        self.makers = makers

    def __getitem__(self, name):
        return self.makers[name]()


def silu(v):
    return v * jax.nn.sigmoid(v)


def nt_dot(lhs, rhs_t):
    return lax.dot_general(lhs, rhs_t, (((1,), (1,)), ((), ())), preferred_element_type=F32)


def mm(lhs, rhs):
    return jnp.dot(lhs, rhs, preferred_element_type=F32)


def layer_kernel(
    x_hbm, h_hbm, ids_hbm, wg_hbm, wu_hbm, wd_hbm, w_out_hbm,
    conv_ref, w_in_ref, vec_ref, chan_ref, w_xp_ref, w_dt_ref, a_log_ref, w_router_ref,
    y_hbm, h_out_hbm, conv_out_ref,
    xbuf, hbuf, idbuf, wg, wu, wd, w_xp2, w_dt2, a2,
    zbuf, xcbuf, dbuf, pnbuf,
    p_part, p_r0, p_s1, p_r1, p_s2, p_r2, p_sum,
    yg_all, wo_all, ubuf, mbuf, qbuf, acc, prob,
    y_part, y_r0, y_s1, y_r1, y_s2, y_r2, ybuf,
    in_sem, h_sem, out_sem, p_send, p_recv, y_send, y_recv, g_send, g_recv,
):
    steps, batch, d_model = x_hbm.shape
    state_dim, inner = a_log_ref.shape
    dt_rank = w_dt_ref.shape[0]
    p_dim = w_xp_ref.shape[0]
    experts = wg_hbm.shape[0]
    f_loc = wg_hbm.shape[2]
    rows = CHUNK_ROWS
    chunks = batch // rows
    tokens = steps * rows
    half_rows = tokens // 2

    tp = lax.axis_index("tp")
    core = tp % 2
    chip = tp // 2
    other = 1 - core
    chip_a = chip + 1 - 2 * (chip % 2)
    chip_b = 3 - chip
    chip_far = (chip + 2) % 4
    mate = {"tp": 2 * chip + other}
    peer_a = {"tp": 2 * chip_a + core}
    peer_b = {"tp": 2 * chip_b + core}

    def copy_to(src, dst, send_sem, recv_sem, peer):
        return pltpu.make_async_remote_copy(
            src_ref=src, dst_ref=dst, send_sem=send_sem, recv_sem=recv_sem, device_id=peer, device_id_type=pl.DeviceIdType.MESH
        )

    in_copies = [
        pltpu.make_async_copy(x_hbm, xbuf, in_sem.at[0]),
        pltpu.make_async_copy(ids_hbm, idbuf, in_sem.at[1]),
        pltpu.make_async_copy(wg_hbm, wg, in_sem.at[2]),
        pltpu.make_async_copy(wu_hbm, wu, in_sem.at[3]),
        pltpu.make_async_copy(wd_hbm, wd, in_sem.at[4]),
    ]
    h_in = pltpu.make_async_copy(h_hbm, hbuf, h_sem.at[0])
    wo_in = pltpu.make_async_copy(w_out_hbm, wo_all.at[pl.ds(pl.multiple_of((core * 4 + chip) * inner, inner), inner), :], in_sem.at[5])
    in_copies[0].start()
    wo_in.start()
    h_in.start()
    for cp in in_copies[1:]:
        cp.start()

    barrier = pltpu.get_barrier_semaphore()
    for peer in (mate, peer_a, peer_b):
        pl.semaphore_signal(barrier, inc=1, device_id=peer, device_id_type=pl.DeviceIdType.MESH)
    pl.semaphore_wait(barrier, 3)

    def wo_block(c, x):
        return wo_all, lambda lo, n: (pl.ds(pl.multiple_of((c * 4 + x) * inner + lo, n), n), slice(None)), inner

    def yg_block(ch):
        def block(c, x):
            col = pl.ds(pl.multiple_of((c * 4 + x) * inner, inner), inner)
            return yg_all, lambda lo, n: (ch, pl.ds(lo, n), col), tokens
        return block

    def ag_copies(block, k):
        def cut(c, x, part=None):
            ref, index, n = block(c, x)
            if part is None:
                return ref.at[index(0, n)]
            return ref.at[index(part * (n // 2), n // 2)]

        def make(idx, src, peer, part=None):
            return copy_to(cut(core, src, part), cut(core, src, part), g_send.at[k, idx], g_recv.at[k, idx], peer)

        def take(idx, c, src, part=None):
            return copy_to(cut(c, src, part), cut(c, src, part), g_send.at[k, idx], g_recv.at[k, idx], mate)

        sends = Lazy(
            own_a=lambda: make(0, chip, peer_a), own_b=lambda: make(1, chip, peer_b),
            fwd_b=lambda: make(2, chip_a, peer_b, 0), fwd_a=lambda: make(3, chip_b, peer_a, 1),
            m_own=lambda: make(4, chip, mate), m_a=lambda: make(5, chip_a, mate),
            m_b=lambda: make(6, chip_b, mate), m_far=lambda: make(7, chip_far, mate),
        )
        recvs = Lazy(
            a=lambda: take(0, core, chip_a), b=lambda: take(1, core, chip_b),
            far0=lambda: take(2, core, chip_far, 0), far1=lambda: take(3, core, chip_far, 1),
            m_own=lambda: take(4, other, chip), m_a=lambda: take(5, other, chip_a),
            m_b=lambda: take(6, other, chip_b), m_far=lambda: take(7, other, chip_far),
        )
        return sends, recvs

    def ag_first(block, k):
        s, _ = ag_copies(block, k)
        s["own_a"].start()
        s["own_b"].start()
        s["m_own"].start()

    def ag_relay(block, k):
        s, r = ag_copies(block, k)
        r["a"].wait_recv()
        s["fwd_b"].start()
        s["m_a"].start()
        r["b"].wait_recv()
        s["fwd_a"].start()
        s["m_b"].start()

    def ag_far(block, k):
        s, r = ag_copies(block, k)
        r["far0"].wait_recv()
        r["far1"].wait_recv()
        s["m_far"].start()

    def ag_done(block, k):
        _, r = ag_copies(block, k)
        for name in ("m_own", "m_a", "m_b", "m_far"):
            r[name].wait_recv()

    def ag_drain(block, k):
        s, _ = ag_copies(block, k)
        for name in ("own_a", "own_b", "fwd_b", "fwd_a", "m_own", "m_a", "m_b", "m_far"):
            s[name].wait_send()

    def ar_copies(part, r0, s1, r1, s2, r2, total, send, recv, ch, n):
        q = n // 4
        keep = pl.ds(pl.multiple_of(core * (n // 2), n // 2), n // 2)
        give = pl.ds(pl.multiple_of(other * (n // 2), n // 2), n // 2)
        lo, hi = pl.ds(0, q), pl.ds(q, q)

        def make(idx, src, dst, peer):
            return copy_to(src, dst, send.at[ch, idx], recv.at[ch, idx], peer)

        return Lazy(
            swap=lambda: make(0, part.at[ch, give], r0.at[ch], mate),
            a1=lambda: make(1, s1.at[ch, lo], r1.at[ch, lo], peer_a), b1=lambda: make(2, s1.at[ch, hi], r1.at[ch, hi], peer_b),
            a2=lambda: make(3, s2.at[ch, lo], r2.at[ch, lo], peer_b), b2=lambda: make(4, s2.at[ch, hi], r2.at[ch, hi], peer_a),
            out=lambda: make(5, total.at[ch, keep], total.at[ch, keep], mate),
            back=lambda: make(5, total.at[ch, give], total.at[ch, give], mate),
        ), keep

    def p_ar(ch):
        return ar_copies(p_part, p_r0, p_s1, p_r1, p_s2, p_r2, p_sum, p_send, p_recv, ch, half_rows)

    def y_ar(ch):
        return ar_copies(y_part, y_r0, y_s1, y_r1, y_s2, y_r2, ybuf, y_send, y_recv, ch, tokens)

    def ar_one(cs, keep, part, r0, s1, ch):
        cs["swap"].wait_recv()
        s1[ch] = (part[ch, keep].astype(F32) + r0[ch].astype(F32)).astype(s1.dtype)
        cs["a1"].start()
        cs["b1"].start()

    def ar_two(cs, s1, r1, s2, ch):
        cs["a1"].wait_recv()
        cs["b1"].wait_recv()
        s2[ch] = (s1[ch].astype(F32) + r1[ch].astype(F32)).astype(s2.dtype)
        cs["a2"].start()
        cs["b2"].start()

    def p_one(ch):
        cs, keep = p_ar(ch)
        ar_one(cs, keep, p_part, p_r0, p_s1, ch)

    def p_two(ch):
        cs, _ = p_ar(ch)
        ar_two(cs, p_s1, p_r1, p_s2, ch)

    def p_three(ch):
        cs, keep = p_ar(ch)
        cs["a2"].wait_recv()
        cs["b2"].wait_recv()
        p_sum[ch, keep] = p_s2[ch] + p_r2[ch]
        cs["out"].start()

    def y_one(ch):
        cs, keep = y_ar(ch)
        ar_one(cs, keep, y_part, y_r0, y_s1, ch)

    def y_two(ch):
        cs, _ = y_ar(ch)
        ar_two(cs, y_s1, y_r1, y_s2, ch)

    def y_three(ch):
        cs, keep = y_ar(ch)
        cs["a2"].wait_recv()
        cs["b2"].wait_recv()
        moe_sum = y_s2[ch].astype(F32) + y_r2[ch].astype(F32)
        ybuf[ch, keep] = (ubuf[ch, keep].astype(F32) + moe_sum).astype(BF16)
        cs["out"].start()

    def y_out(ch):
        return [
            pltpu.make_async_copy(
                ybuf.at[ch, pl.ds(s * rows, rows)], y_hbm.at[s, pl.ds(pl.multiple_of(ch * rows, rows), rows)], out_sem.at[1 + s, ch]
            )
            for s in range(steps)
        ]

    def y_four(ch):
        cs, _ = y_ar(ch)
        cs["back"].wait_recv()
        for cp in y_out(ch):
            cp.start()

    def h_out(ch):
        n = rows * state_dim
        part = pl.ds(pl.multiple_of(ch * n, n), n)
        return pltpu.make_async_copy(hbuf.at[part], h_out_hbm.at[part], out_sem.at[0, ch])

    def chunk_rows(ch):
        return pl.ds(pl.multiple_of(ch * rows, rows), rows)

    def stage_in(ch):
        xf = xbuf[:, chunk_rows(ch), :].reshape(tokens, d_model).astype(F32)
        scale = lax.rsqrt(jnp.mean(xf * xf, axis=-1, keepdims=True) + EPSILON)
        norm = (xf * scale * vec_ref[0:1, :]).astype(BF16)
        proj = mm(norm, w_in_ref[...]).astype(BF16)
        zbuf[ch] = proj[:, inner:]
        xi = proj[:, :inner]
        win = [conv_ref[j, chunk_rows(ch), :].astype(F32) for j in range(3)]
        win += [xi[s * rows:(s + 1) * rows].astype(F32) for s in range(steps)]
        for s in range(steps):
            pre = chan_ref[4:5, :]
            for j in range(4):
                pre = pre + win[s + j] * chan_ref[j:j + 1, :]
            lane = (s // 2) * inner
            xcbuf[ch, (s % 2) * rows:(s % 2 + 1) * rows, lane:lane + inner] = silu(pre).astype(BF16)
        for j in range(3):
            conv_out_ref[j, chunk_rows(ch), :] = xi[(j + 1) * rows:(j + 2) * rows]
        p_part[ch] = nt_dot(xcbuf[ch], w_xp2[...])
        cs, _ = p_ar(ch)
        cs["swap"].start()

    def stage_ssm(ch):
        cs, _ = p_ar(ch)
        cs["back"].wait_recv()
        p = p_sum[ch]
        lane = lax.broadcasted_iota(jnp.int32, p.shape, 1)
        sq = p * p
        mean = jnp.zeros_like(p)
        for base in (0, p_dim):
            for lo, n in ((0, dt_rank), (dt_rank, state_dim), (dt_rank + state_dim, state_dim)):
                inside = (lane >= base + lo) & (lane < base + lo + n)
                total = jnp.sum(jnp.where(inside, sq, 0.0), axis=-1, keepdims=True) * (1.0 / n)
                mean = jnp.where(inside, total, mean)
        pn = p * lax.rsqrt(mean + EPSILON) * chan_ref[7:8, :]
        pnbuf[...] = pn
        pre = mm(pn.astype(BF16), w_dt2[...])
        bias = chan_ref[5:6, :]
        pre = pre + jnp.concatenate([bias, bias], axis=1)
        dbuf[...] = jnp.maximum(pre, 0.0) + jnp.log1p(jnp.exp(-jnp.abs(pre)))
        my_col = pl.ds(pl.multiple_of((core * 4 + chip) * inner, inner), inner)
        tile = 16

        def tile_body(bt, carry):
            r0 = pl.multiple_of(bt * tile, tile)
            d, dx, y, pns = [], [], [], []
            for s in range(steps):
                at = pl.ds(pl.multiple_of((s % 2) * rows + r0, tile), tile)
                cols = slice((s // 2) * inner, (s // 2 + 1) * inner)
                ds_ = dbuf[at, cols]
                xc = xcbuf[ch, at, cols].astype(F32)
                d.append(ds_)
                dx.append(ds_ * xc)
                y.append(chan_ref[6:7, :] * xc)
                pns.append(pnbuf[at, :])
            for n in range(state_dim):
                where = pl.ds((ch * rows + r0) * state_dim + n, tile, stride=state_dim)
                h = hbuf[where, :]
                a_n = a2[n:n + 1, :]
                for s in range(steps):
                    kb = (s // 2) * p_dim + dt_rank + n
                    kc = kb + state_dim
                    bvec = pns[s][:, kb:kb + 1]
                    cvec = pns[s][:, kc:kc + 1]
                    h = jnp.exp2(d[s] * a_n) * h + dx[s] * bvec
                    y[s] = y[s] + h * cvec
                hbuf[where, :] = h
            for s in range(steps):
                at = pl.ds(pl.multiple_of(s * rows + r0, tile), tile)
                z = zbuf[ch, at, :].astype(F32)
                yg_all[ch, at, my_col] = (y[s] * silu(z)).astype(BF16)
            return carry

        lax.fori_loop(0, rows // tile, tile_body, 0)
        h_out(ch).start()
        ag_first(yg_block(ch), ch)

    def stage_mid(ch):
        ag_done(yg_block(ch), ch)
        mix = mm(yg_all[ch], wo_all[...])
        xf = xbuf[:, chunk_rows(ch), :].reshape(tokens, d_model).astype(F32)
        u = (xf + mix).astype(BF16)
        ubuf[ch] = u
        uf = u.astype(F32)
        scale = lax.rsqrt(jnp.mean(uf * uf, axis=-1, keepdims=True) + EPSILON)
        m = (uf * scale * vec_ref[1:2, :]).astype(BF16)
        mbuf[...] = m
        logits = nt_dot(m, w_router_ref[...])
        peak = jnp.max(logits, axis=-1, keepdims=True)
        ex = jnp.exp(logits - peak)
        ids = idbuf[:, chunk_rows(ch), 0:experts].reshape(tokens, experts)
        hit = ids == lax.broadcasted_iota(jnp.int32, (tokens, experts), 1)
        chosen = jnp.sum(jnp.where(hit, ex, 0.0), axis=-1, keepdims=True) / jnp.sum(ex, axis=-1, keepdims=True)
        prob[...] = jnp.broadcast_to(chosen, prob.shape)

    def stage_experts(ch, g):
        m = mbuf[...]
        ids = idbuf[:, chunk_rows(ch), :].reshape(tokens, inner)
        ids = jnp.concatenate([ids] * (f_loc // inner), axis=1)
        for j in range(GROUP):
            e = g * GROUP + j
            q = silu(mm(m, wg[e])) * mm(m, wu[e])
            qbuf[:, j * f_loc:(j + 1) * f_loc] = jnp.where(ids == e, q, 0.0).astype(BF16)
        part = mm(qbuf[...], wd[g * GROUP * f_loc:(g + 1) * GROUP * f_loc, :])
        if g == 0:
            acc[...] = part
        elif g < experts // GROUP - 1:
            acc[...] += part
        else:
            total = acc[...] + part
            weight = jnp.concatenate([prob[...]] * (d_model // inner), axis=1)
            y_part[ch] = (total * weight).astype(BF16)
            cs, _ = y_ar(ch)
            cs["swap"].start()

    def when_chunk(ch, fn):
        pl.when((ch >= 0) & (ch < chunks))(lambda: fn(ch))

    def loop(n, body):
        def step(i, carry):
            body(i)
            return carry
        lax.fori_loop(0, n, step, 0)

    wo_in.wait()
    ag_first(wo_block, chunks)
    w_xp2[...] = jnp.zeros_like(w_xp2)
    w_dt2[...] = jnp.zeros_like(w_dt2)
    for k in range(2):
        w_xp2[k * p_dim:(k + 1) * p_dim, k * inner:(k + 1) * inner] = w_xp_ref[...]
        w_dt2[k * p_dim:k * p_dim + dt_rank, k * inner:(k + 1) * inner] = w_dt_ref[...]
    a2[...] = jnp.exp(a_log_ref[...]) * (-LOG2E)
    in_copies[0].wait()

    def first_body(t):
        stage_in(t)
        when_chunk(t - 2, p_one)

    loop(chunks, first_body)
    p_one(chunks - 2)
    p_one(chunks - 1)
    for ch in range(4):
        p_two(ch)
    ag_relay(wo_block, chunks)
    for ch in range(4, chunks):
        p_two(ch)
    for ch in range(3):
        p_three(ch)
    h_in.wait()

    def ssm_body(t):
        stage_ssm(t)
        when_chunk(t + 3, p_three)
        when_chunk(t - 4, lambda ch: ag_relay(yg_block(ch), ch))
        when_chunk(t - 6, lambda ch: ag_far(yg_block(ch), ch))

    loop(chunks, ssm_body)
    ag_far(wo_block, chunks)
    for cp in in_copies[1:]:
        cp.wait()
    ag_done(wo_block, chunks)

    def moe_body(t):
        stage_mid(t)
        for g in range(experts // GROUP):
            stage_experts(t, g)
            if g == 0:
                when_chunk(t + 4, lambda ch: ag_relay(yg_block(ch), ch))
                when_chunk(t - 2, y_two)
            elif g == 1:
                when_chunk(t + 2, lambda ch: ag_far(yg_block(ch), ch))
                when_chunk(t - 1, y_one)
            elif g == 2:
                when_chunk(t - 3, y_three)
            else:
                when_chunk(t - 4, y_four)

    loop(chunks, moe_body)
    last = chunks - 1
    y_two(last - 1)
    y_three(last - 2)
    y_one(last)
    y_four(last - 3)
    y_three(last - 1)
    y_two(last)
    y_four(last - 2)
    y_four(last - 1)
    y_three(last)
    y_four(last)

    def drain(ch):
        h_out(ch).wait()
        for cp in y_out(ch):
            cp.wait()
        ag_drain(yg_block(ch), ch)
        for cs, _ in (p_ar(ch), y_ar(ch)):
            for name in ("swap", "a1", "b1", "a2", "b2", "out"):
                cs[name].wait_send()

    loop(chunks, drain)
    ag_drain(wo_block, chunks)


def solution(mesh):
    act_spec = P(None, "dp", None)
    state_spec = P("dp", "tp", None)
    in_specs = (act_spec, state_spec, state_spec, act_spec, P(None), P(None, None, "tp"), P("tp", None), P("tp"), P("tp", None), P(None), P(None), P(None), P(None, "tp"), P("tp"), P("tp", None), P("tp"), P("tp", None), P(None), P(None, None), P(None, None, "tp"), P(None, None, "tp"), P(None, "tp", None))
    out_specs = (act_spec, state_spec, state_spec)

    def layer_steps(x_steps, conv_state, ssm_state, expert_ids, g_in, w_in, conv_w, conv_b, w_xp, g_dt, g_b, g_c, w_dt, b_dt, a_log, d_skip, w_out, g_ff, w_router, w_gate, w_up, w_down):
        steps, batch, d_model = x_steps.shape
        inner = w_in.shape[2]
        state_dim = a_log.shape[1]
        experts, _, f_loc = w_gate.shape
        p_dim = w_xp.shape[1]
        rows = CHUNK_ROWS
        chunks = batch // rows
        tokens = steps * rows
        group_inner = w_out.shape[0] * mesh.shape["tp"]

        w_in2 = w_in.reshape(d_model, 2 * inner)
        vec = jnp.stack([g_in, g_ff]).astype(F32)
        gains = jnp.concatenate([g_dt, g_b, g_c]).astype(F32)
        chan = jnp.concatenate([
            conv_w.T.astype(F32),
            jnp.stack([conv_b.astype(F32), b_dt.astype(F32), d_skip, jnp.concatenate([gains, gains])]),
        ])
        ids = jnp.broadcast_to(expert_ids, (steps, batch, inner))
        h_flat = jnp.swapaxes(ssm_state, 1, 2).reshape(batch * state_dim, inner)
        conv_t = jnp.transpose(conv_state, (2, 0, 1))

        any_spec = pl.BlockSpec(memory_space=pl.ANY)
        vmem_spec = pl.BlockSpec(memory_space=pltpu.VMEM)
        half = tokens // 2
        p_half = (chunks, half // 2, 2 * p_dim)
        y_half = (chunks, half, d_model)
        dma = pltpu.SemaphoreType.DMA
        scratch = [
            pltpu.VMEM(x_steps.shape, BF16),
            pltpu.VMEM(h_flat.shape, F32),
            pltpu.VMEM(ids.shape, jnp.int32),
            pltpu.VMEM(w_gate.shape, BF16),
            pltpu.VMEM(w_up.shape, BF16),
            pltpu.VMEM((experts * f_loc, d_model), BF16),
            pltpu.VMEM((2 * p_dim, 2 * inner), BF16),
            pltpu.VMEM((2 * p_dim, 2 * inner), BF16),
            pltpu.VMEM((state_dim, inner), F32),
            pltpu.VMEM((chunks, tokens, inner), BF16),
            pltpu.VMEM((chunks, half, 2 * inner), BF16),
            pltpu.VMEM((half, 2 * inner), F32),
            pltpu.VMEM((half, 2 * p_dim), F32),
            pltpu.VMEM((chunks, half, 2 * p_dim), F32),
            pltpu.VMEM(p_half, F32),
            pltpu.VMEM(p_half, F32),
            pltpu.VMEM(p_half, F32),
            pltpu.VMEM(p_half, F32),
            pltpu.VMEM(p_half, F32),
            pltpu.VMEM((chunks, half, 2 * p_dim), F32),
            pltpu.VMEM((chunks, tokens, group_inner), BF16),
            pltpu.VMEM((group_inner, d_model), BF16),
            pltpu.VMEM((chunks, tokens, d_model), BF16),
            pltpu.VMEM((tokens, d_model), BF16),
            pltpu.VMEM((tokens, GROUP * f_loc), BF16),
            pltpu.VMEM((tokens, d_model), F32),
            pltpu.VMEM((tokens, inner), F32),
            pltpu.VMEM((chunks, tokens, d_model), BF16),
            pltpu.VMEM(y_half, BF16),
            pltpu.VMEM(y_half, BF16),
            pltpu.VMEM(y_half, BF16),
            pltpu.VMEM(y_half, BF16),
            pltpu.VMEM(y_half, BF16),
            pltpu.VMEM((chunks, tokens, d_model), BF16),
            dma((6,)),
            dma((1,)),
            dma((1 + steps, chunks)),
            dma((chunks, 6)),
            dma((chunks, 6)),
            dma((chunks, 6)),
            dma((chunks, 6)),
            dma((chunks + 1, 8)),
            dma((chunks + 1, 8)),
        ]
        y, h_new, conv_new = pl.pallas_call(
            layer_kernel,
            out_shape=(
                jax.ShapeDtypeStruct(x_steps.shape, BF16),
                jax.ShapeDtypeStruct(h_flat.shape, F32),
                jax.ShapeDtypeStruct(conv_t.shape, BF16),
            ),
            in_specs=[any_spec] * 7 + [vmem_spec] * 8,
            out_specs=(any_spec, any_spec, vmem_spec),
            scratch_shapes=scratch,
            compiler_params=pltpu.CompilerParams(collective_id=0, has_side_effects=True, vmem_limit_bytes=60 * 1024 * 1024),
        )(x_steps, h_flat, ids, w_gate, w_up, w_down.reshape(experts * f_loc, d_model), w_out, conv_t, w_in2, vec, chan, w_xp.T, w_dt, a_log.T, w_router.T)
        h_new = jnp.swapaxes(h_new.reshape(batch, state_dim, inner), 1, 2)
        return y, jnp.transpose(conv_new, (1, 2, 0)), h_new

    return jax.shard_map(layer_steps, mesh=mesh, in_specs=in_specs, out_specs=out_specs, check_vma=False)
```

time: 464 us -> 113 us (0.24)
  the two profiles are of different devices: /device:TPU:112 before, /device:TPU:113 now
where the time goes in v1:
time: 113 us
  Pallas kernels  92.1 us (82%)
  local copies, waits for them, and re-layouts  17.4 us (15%)
  other arithmetic  2.6 us (2%)
    pallas_call x1, Pallas kernels, layer_steps(): pl.pallas_call(layer_kernel, out_shape=(jax.ShapeDtypeStruct(x_steps.shap...  92.1 us
    unnamed x7, local copies, waits for them, and re-layouts  9.37 us
    concatenate x1, local copies, waits for them, and re-layouts, layer_steps(): jnp.concatenate([gains, gains])  4.1 us

profile of v1, /device:TPU:113, one launch (start us, length us, event | category | flops | bytes accessed | tf_op | source)
XLA Modules:
  0.0 112.7 jit_solution(7730781538614822857)
XLA Ops:
  0.6 0.7 bitcast_convert_fusion.2
  1.3 4.1 %concatenate.9 = bf16[128]{0:T(256)(128)(2,1)S(1)} concatenate(bf16[32]{0:T(256)(128)(2,1)} %param.31, bf16[16]{0:T(256)(128)(2,1)} %param.32, bf16[16]{0:T(256)(128)(2,1)} %param.33, bf16[32]{0:T(256)(128)(2,1)} %param.31, bf16[16]{0:T(256)(128)(2,1)} %param.32, bf16[16]{0:T(256)(128)(2,1)} %param.33), dimensions={0} | concatenate | bytes 512 | tf_op jit(solution)/shard_map/concatenate | solution.py:477
  5.4 0.7 bitcast_convert_fusion
  6.0 0.7 stack.30
  6.7 0.7 convert_bitcast_fusion
  7.4 1.3 %concatenate.10.chan_ref = f32[8,128]{1,0:T(8,128)} concatenate(f32[4,128]{1,0:T(4,128)S(1)} %convert_bitcast_fusion, f32[1,128]{1,0:T(1,128)S(1)} %bitcast_convert_fusion.2, f32[1,128]{1,0:T(1,128)S(1)} %get-tuple-element.10, f32[1,128]{1,0:T(1,128)} %bitcast.42, f32[1,128]{1,0:T(1,128)S(1)} %get-tuple-element.9), dimensions={0} | concatenate | bytes 8192 | tf_op jit(solution)/shard_map/concatenate | solution.py:475
  8.7 0.7 stack.31
  9.3 0.6 maximum_convert_fusion.vec_ref
  10.0 0.7 copy.30
  10.7 1.7 %copy.29 = bf16[64,8,2,128]{3,1,2,0:T(8,128)(2,1)} copy(bf16[64,8,2,128]{3,2,1,0:T(2,128)(2,1)} %bitcast.37) | data formatting | bytes 524288
  12.3 1.3 %broadcast_in_dim.8.ids_hbm = s32[4,512,128]{2,1,0:T(8,128)} broadcast(s32[4,512]{1,0:T(4,128)S(1)} %bitcast.38), dimensions={0,1} | broadcast | bytes 1056768 | tf_op jit(solution)/shard_map/broadcast_in_dim | solution.py:479
  13.6 92.1 %shard_map.229 = (bf16[4,512,512]{2,1,0:T(8,128)(2,1)}, f32[8192,128]{1,0:T(8,128)}, bf16[3,512,128]{2,1,0:T(8,128)(2,1)}) custom-call(bf16[4,512,512]{2,1,0:T(8,128)(2,1)} %x_hbm.1, f32[8192,128]{1,0:T(8,128)} %bitcast.32, s32[4,512,128]{2,1,0:T(8,128)} %broadcast_in_dim.8.ids_hbm, bf16[16,512,256]{2,1,0:T(8,128)(2,1)} %wg_hbm.1, ...), custom_call_target="tpu_custom_call" | custom-call | tf_op jit(solution)/shard_map/pallas_call | solution.py:534
  105.7 0.0 copy-start
  105.8 3.2 %copy.34 = bf16[4,512,512]{2,1,0:T(8,128)(2,1)} copy(bf16[4,512,512]{2,1,0:T(8,128)(2,1)} %get-tuple-element.14) | data formatting | bytes 4194304
  109.0 1.8 %copy.35 = bf16[512,128,3]{1,0,2:T(8,128)(2,1)} copy(bf16[512,128,3]{1,0,2:T(8,128)(2,1)} %bitcast.35) | data formatting | bytes 786432
  110.7 0.0 copy-done
  110.7 2.0 %copy.36 = f32[512,128,16]{1,2,0:T(8,128)} copy(f32[512,128,16]{1,2,0:T(8,128)S(1)} %bitcast.31) | data formatting | bytes 8388608
Async XLA Ops:
  105.7 5.0 %copy-start = (f32[8192,128]{1,0:T(8,128)S(1)}, f32[8192,128]{1,0:T(8,128)}, u32[]{:S(2)}) copy-start(f32[8192,128]{1,0:T(8,128)} %get-tuple-element.8) | copy-start | bytes 12582916

commit v2 on v1

--- a/solution.py
+++ b/solution.py
@@ -37,15 +37,16 @@
 
 
 def layer_kernel(
-    x_hbm, h_hbm, ids_hbm, wg_hbm, wu_hbm, wd_hbm, w_out_hbm,
-    conv_ref, w_in_ref, vec_ref, chan_ref, w_xp_ref, w_dt_ref, a_log_ref, w_router_ref,
-    y_hbm, h_out_hbm, conv_out_ref,
-    xbuf, hbuf, idbuf, wg, wu, wd, w_xp2, w_dt2, a2,
-    zbuf, xcbuf, dbuf, pnbuf,
+    x_hbm, h_hbm, wg_hbm, wu_hbm, wd_hbm, w_out_hbm,
+    ids_ref, conv_ref, w_in_ref, g_in_ref, g_ff_ref, conv_w_ref, conv_b_ref, b_dt_ref, d_skip_ref,
+    g_dt_ref, g_b_ref, g_c_ref, w_xp_ref, w_dt_ref, a_log_ref, w_router_ref,
+    y_ref, h_ref, conv_out_ref,
+    xbuf, hbuf, idbuf, wg, wu, wd, w_in2, w_tmp, vec_ref, chan_ref, w_xp2, w_dt2, a2, spread,
+    zbuf, xcbuf, dbuf, pnbuf, bbuf, cbuf,
     p_part, p_r0, p_s1, p_r1, p_s2, p_r2, p_sum,
     yg_all, wo_all, ubuf, mbuf, qbuf, acc, prob,
-    y_part, y_r0, y_s1, y_r1, y_s2, y_r2, ybuf,
-    in_sem, h_sem, out_sem, p_send, p_recv, y_send, y_recv, g_send, g_recv,
+    y_part, y_r0, y_s1, y_r1, y_s2, y_r2,
+    in_sem, p_send, p_recv, y_send, y_recv, g_send, g_recv,
 ):
     steps, batch, d_model = x_hbm.shape
     state_dim, inner = a_log_ref.shape
@@ -74,20 +75,13 @@
             src_ref=src, dst_ref=dst, send_sem=send_sem, recv_sem=recv_sem, device_id=peer, device_id_type=pl.DeviceIdType.MESH
         )
 
-    in_copies = [
-        pltpu.make_async_copy(x_hbm, xbuf, in_sem.at[0]),
-        pltpu.make_async_copy(ids_hbm, idbuf, in_sem.at[1]),
-        pltpu.make_async_copy(wg_hbm, wg, in_sem.at[2]),
-        pltpu.make_async_copy(wu_hbm, wu, in_sem.at[3]),
-        pltpu.make_async_copy(wd_hbm, wd, in_sem.at[4]),
-    ]
-    h_in = pltpu.make_async_copy(h_hbm, hbuf, h_sem.at[0])
-    wo_in = pltpu.make_async_copy(w_out_hbm, wo_all.at[pl.ds(pl.multiple_of((core * 4 + chip) * inner, inner), inner), :], in_sem.at[5])
-    in_copies[0].start()
+    x_in = pltpu.make_async_copy(x_hbm, xbuf, in_sem.at[0])
+    h_in = pltpu.make_async_copy(h_hbm, hbuf, in_sem.at[1])
+    w_ins = [pltpu.make_async_copy(src, dst, in_sem.at[2 + i]) for i, (src, dst) in enumerate(((wg_hbm, wg), (wu_hbm, wu), (wd_hbm, wd)))]
+    my_rows = pl.ds(pl.multiple_of((core * 4 + chip) * inner, inner), inner)
+    wo_in = pltpu.make_async_copy(w_out_hbm, wo_all.at[my_rows, :], in_sem.at[5])
+    x_in.start()
     wo_in.start()
-    h_in.start()
-    for cp in in_copies[1:]:
-        cp.start()
 
     barrier = pltpu.get_barrier_semaphore()
     for peer in (mate, peer_a, peer_b):
@@ -130,6 +124,10 @@
         )
         return sends, recvs
 
+    def wo_first():
+        for idx, peer in ((0, peer_a), (1, peer_b), (4, mate)):
+            copy_to(w_out_hbm, wo_all.at[my_rows, :], g_send.at[chunks, idx], g_recv.at[chunks, idx], peer).start()
+
     def ag_first(block, k):
         s, _ = ag_copies(block, k)
         s["own_a"].start()
@@ -161,7 +159,7 @@
         for name in ("own_a", "own_b", "fwd_b", "fwd_a", "m_own", "m_a", "m_b", "m_far"):
             s[name].wait_send()
 
-    def ar_copies(part, r0, s1, r1, s2, r2, total, send, recv, ch, n):
+    def ar_copies(part, r0, s1, r1, s2, r2, total_keep, total_give, send, recv, ch, n):
         q = n // 4
         keep = pl.ds(pl.multiple_of(core * (n // 2), n // 2), n // 2)
         give = pl.ds(pl.multiple_of(other * (n // 2), n // 2), n // 2)
@@ -174,15 +172,19 @@
             swap=lambda: make(0, part.at[ch, give], r0.at[ch], mate),
             a1=lambda: make(1, s1.at[ch, lo], r1.at[ch, lo], peer_a), b1=lambda: make(2, s1.at[ch, hi], r1.at[ch, hi], peer_b),
             a2=lambda: make(3, s2.at[ch, lo], r2.at[ch, lo], peer_b), b2=lambda: make(4, s2.at[ch, hi], r2.at[ch, hi], peer_a),
-            out=lambda: make(5, total.at[ch, keep], total.at[ch, keep], mate),
-            back=lambda: make(5, total.at[ch, give], total.at[ch, give], mate),
+            out=lambda: make(5, total_keep(), total_keep(), mate),
+            back=lambda: make(5, total_give(), total_give(), mate),
         ), keep
 
     def p_ar(ch):
-        return ar_copies(p_part, p_r0, p_s1, p_r1, p_s2, p_r2, p_sum, p_send, p_recv, ch, half_rows)
+        def total(c):
+            return lambda: p_sum.at[ch, pl.ds(pl.multiple_of(c * (half_rows // 2), half_rows // 2), half_rows // 2)]
+        return ar_copies(p_part, p_r0, p_s1, p_r1, p_s2, p_r2, total(core), total(other), p_send, p_recv, ch, half_rows)
 
     def y_ar(ch):
-        return ar_copies(y_part, y_r0, y_s1, y_r1, y_s2, y_r2, ybuf, y_send, y_recv, ch, tokens)
+        def total(c):
+            return lambda: y_ref.at[pl.ds(c * (steps // 2), steps // 2), chunk_rows(ch)]
+        return ar_copies(y_part, y_r0, y_s1, y_r1, y_s2, y_r2, total(core), total(other), y_send, y_recv, ch, tokens)
 
     def ar_one(cs, keep, part, r0, s1, ch):
         cs["swap"].wait_recv()
@@ -225,27 +227,13 @@
         cs["a2"].wait_recv()
         cs["b2"].wait_recv()
         moe_sum = y_s2[ch].astype(F32) + y_r2[ch].astype(F32)
-        ybuf[ch, keep] = (ubuf[ch, keep].astype(F32) + moe_sum).astype(BF16)
+        y_new = (ubuf[ch, keep].astype(F32) + moe_sum).astype(BF16)
+        y_ref[pl.ds(core * (steps // 2), steps // 2), chunk_rows(ch), :] = y_new.reshape(steps // 2, rows, d_model)
         cs["out"].start()
-
-    def y_out(ch):
-        return [
-            pltpu.make_async_copy(
-                ybuf.at[ch, pl.ds(s * rows, rows)], y_hbm.at[s, pl.ds(pl.multiple_of(ch * rows, rows), rows)], out_sem.at[1 + s, ch]
-            )
-            for s in range(steps)
-        ]
 
     def y_four(ch):
         cs, _ = y_ar(ch)
         cs["back"].wait_recv()
-        for cp in y_out(ch):
-            cp.start()
-
-    def h_out(ch):
-        n = rows * state_dim
-        part = pl.ds(pl.multiple_of(ch * n, n), n)
-        return pltpu.make_async_copy(hbuf.at[part], h_out_hbm.at[part], out_sem.at[0, ch])
 
     def chunk_rows(ch):
         return pl.ds(pl.multiple_of(ch * rows, rows), rows)
@@ -254,7 +242,7 @@
         xf = xbuf[:, chunk_rows(ch), :].reshape(tokens, d_model).astype(F32)
         scale = lax.rsqrt(jnp.mean(xf * xf, axis=-1, keepdims=True) + EPSILON)
         norm = (xf * scale * vec_ref[0:1, :]).astype(BF16)
-        proj = mm(norm, w_in_ref[...]).astype(BF16)
+        proj = mm(norm, w_in2[...]).astype(BF16)
         zbuf[ch] = proj[:, inner:]
         xi = proj[:, :inner]
         win = [conv_ref[j, chunk_rows(ch), :].astype(F32) for j in range(3)]
@@ -285,6 +273,17 @@
                 mean = jnp.where(inside, total, mean)
         pn = p * lax.rsqrt(mean + EPSILON) * chan_ref[7:8, :]
         pnbuf[...] = pn
+        low = dt_rank + state_dim
+        is_c = (lane % p_dim) >= low
+        first = pn.astype(BF16).astype(F32)
+        second = (pn - first).astype(BF16).astype(F32)
+        third = pn - first - second
+        parts = [jnp.where(is_c, v, 0.0) for v in (first, second, third)]
+        split = parts[0] + pltpu.roll(parts[1], state_dim, 1) + pltpu.roll(parts[2], 2 * state_dim, 1)
+        cbuf[...] = mm(split.astype(BF16), spread[...])
+        for k in range(2 * state_dim):
+            at = (k // state_dim) * p_dim + dt_rank + k % state_dim
+            bbuf[:, k * inner:(k + 1) * inner] = jnp.broadcast_to(pn[:, at:at + 1], (half_rows, inner))
         pre = mm(pn.astype(BF16), w_dt2[...])
         bias = chan_ref[5:6, :]
         pre = pre + jnp.concatenate([bias, bias], axis=1)
@@ -294,7 +293,7 @@
 
         def tile_body(bt, carry):
             r0 = pl.multiple_of(bt * tile, tile)
-            d, dx, y, pns = [], [], [], []
+            d, dx, y, ats = [], [], [], []
             for s in range(steps):
                 at = pl.ds(pl.multiple_of((s % 2) * rows + r0, tile), tile)
                 cols = slice((s // 2) * inner, (s // 2 + 1) * inner)
@@ -303,19 +302,16 @@
                 d.append(ds_)
                 dx.append(ds_ * xc)
                 y.append(chan_ref[6:7, :] * xc)
-                pns.append(pnbuf[at, :])
+                ats.append(at)
             for n in range(state_dim):
                 where = pl.ds((ch * rows + r0) * state_dim + n, tile, stride=state_dim)
                 h = hbuf[where, :]
                 a_n = a2[n:n + 1, :]
                 for s in range(steps):
-                    kb = (s // 2) * p_dim + dt_rank + n
-                    kc = kb + state_dim
-                    bvec = pns[s][:, kb:kb + 1]
-                    cvec = pns[s][:, kc:kc + 1]
-                    h = jnp.exp2(d[s] * a_n) * h + dx[s] * bvec
-                    y[s] = y[s] + h * cvec
-                hbuf[where, :] = h
+                    k = (s // 2) * state_dim + n
+                    h = jnp.exp2(d[s] * a_n) * h + dx[s] * bbuf[ats[s], k * inner:(k + 1) * inner]
+                    y[s] = y[s] + h * cbuf[ats[s], k * inner:(k + 1) * inner]
+                h_ref[where, :] = h
             for s in range(steps):
                 at = pl.ds(pl.multiple_of(s * rows + r0, tile), tile)
                 z = zbuf[ch, at, :].astype(F32)
@@ -323,7 +319,6 @@
             return carry
 
         lax.fori_loop(0, rows // tile, tile_body, 0)
-        h_out(ch).start()
         ag_first(yg_block(ch), ch)
 
     def stage_mid(ch):
@@ -373,15 +368,34 @@
             return carry
         lax.fori_loop(0, n, step, 0)
 
-    wo_in.wait()
-    ag_first(wo_block, chunks)
+    wo_first()
+    for cp in (h_in, *w_ins):
+        cp.start()
     w_xp2[...] = jnp.zeros_like(w_xp2)
     w_dt2[...] = jnp.zeros_like(w_dt2)
     for k in range(2):
         w_xp2[k * p_dim:(k + 1) * p_dim, k * inner:(k + 1) * inner] = w_xp_ref[...]
         w_dt2[k * p_dim:k * p_dim + dt_rank, k * inner:(k + 1) * inner] = w_dt_ref[...]
     a2[...] = jnp.exp(a_log_ref[...]) * (-LOG2E)
-    in_copies[0].wait()
+    w_tmp[...] = w_in_ref[...].astype(F32)
+    for k in range(2):
+        w_in2[:, k * inner:(k + 1) * inner] = w_tmp[pl.ds(k, d_model, stride=2), :].astype(BF16)
+    vec_ref[0:1, :] = g_in_ref[...].astype(F32).reshape(1, d_model)
+    vec_ref[1:2, :] = g_ff_ref[...].astype(F32).reshape(1, d_model)
+    chan_ref[0:4, :] = conv_w_ref[...].astype(F32)
+    chan_ref[4:5, :] = conv_b_ref[...].astype(F32).reshape(1, inner)
+    chan_ref[5:6, :] = b_dt_ref[...].astype(F32).reshape(1, inner)
+    chan_ref[6:7, :] = d_skip_ref[...].reshape(1, inner)
+    gains = [g[...].astype(F32).reshape(1, g.shape[0]) for g in (g_dt_ref, g_b_ref, g_c_ref)]
+    chan_ref[7:8, :] = jnp.concatenate(gains + gains, axis=1)
+    row = lax.broadcasted_iota(jnp.int32, (2 * p_dim, inner), 0)
+    for k in range(2 * state_dim):
+        at = (k // state_dim) * p_dim + dt_rank + state_dim + k % state_dim
+        hit = (row == at) | (row == (at + state_dim) % (2 * p_dim)) | (row == (at + 2 * state_dim) % (2 * p_dim))
+        spread[:, k * inner:(k + 1) * inner] = jnp.where(hit, 1.0, 0.0).astype(BF16)
+    for s in range(steps):
+        idbuf[s] = jnp.broadcast_to(ids_ref[s].astype(F32), (inner, batch)).T.astype(jnp.int32)
+    x_in.wait()
 
     def first_body(t):
         stage_in(t)
@@ -407,7 +421,8 @@
 
     loop(chunks, ssm_body)
     ag_far(wo_block, chunks)
-    for cp in in_copies[1:]:
+    wo_in.wait()
+    for cp in w_ins:
         cp.wait()
     ag_done(wo_block, chunks)
 
@@ -417,32 +432,25 @@
             stage_experts(t, g)
             if g == 0:
                 when_chunk(t + 4, lambda ch: ag_relay(yg_block(ch), ch))
-                when_chunk(t - 2, y_two)
+                when_chunk(t - 4, y_three)
             elif g == 1:
                 when_chunk(t + 2, lambda ch: ag_far(yg_block(ch), ch))
                 when_chunk(t - 1, y_one)
             elif g == 2:
-                when_chunk(t - 3, y_three)
-            else:
-                when_chunk(t - 4, y_four)
+                when_chunk(t - 2, y_two)
 
     loop(chunks, moe_body)
     last = chunks - 1
+    y_three(last - 3)
     y_two(last - 1)
     y_three(last - 2)
     y_one(last)
-    y_four(last - 3)
     y_three(last - 1)
     y_two(last)
-    y_four(last - 2)
-    y_four(last - 1)
     y_three(last)
-    y_four(last)
 
     def drain(ch):
-        h_out(ch).wait()
-        for cp in y_out(ch):
-            cp.wait()
+        y_four(ch)
         ag_drain(yg_block(ch), ch)
         for cs, _ in (p_ar(ch), y_ar(ch)):
             for name in ("swap", "a1", "b1", "a2", "b2", "out"):
@@ -469,14 +477,6 @@
         tokens = steps * rows
         group_inner = w_out.shape[0] * mesh.shape["tp"]
 
-        w_in2 = w_in.reshape(d_model, 2 * inner)
-        vec = jnp.stack([g_in, g_ff]).astype(F32)
-        gains = jnp.concatenate([g_dt, g_b, g_c]).astype(F32)
-        chan = jnp.concatenate([
-            conv_w.T.astype(F32),
-            jnp.stack([conv_b.astype(F32), b_dt.astype(F32), d_skip, jnp.concatenate([gains, gains])]),
-        ])
-        ids = jnp.broadcast_to(expert_ids, (steps, batch, inner))
         h_flat = jnp.swapaxes(ssm_state, 1, 2).reshape(batch * state_dim, inner)
         conv_t = jnp.transpose(conv_state, (2, 0, 1))
 
@@ -489,17 +489,24 @@
         scratch = [
             pltpu.VMEM(x_steps.shape, BF16),
             pltpu.VMEM(h_flat.shape, F32),
-            pltpu.VMEM(ids.shape, jnp.int32),
+            pltpu.VMEM((steps, batch, inner), jnp.int32),
             pltpu.VMEM(w_gate.shape, BF16),
             pltpu.VMEM(w_up.shape, BF16),
             pltpu.VMEM((experts * f_loc, d_model), BF16),
+            pltpu.VMEM((d_model, 2 * inner), BF16),
+            pltpu.VMEM((2 * d_model, inner), F32),
+            pltpu.VMEM((2, d_model), F32),
+            pltpu.VMEM((8, inner), F32),
             pltpu.VMEM((2 * p_dim, 2 * inner), BF16),
             pltpu.VMEM((2 * p_dim, 2 * inner), BF16),
             pltpu.VMEM((state_dim, inner), F32),
+            pltpu.VMEM((2 * p_dim, 2 * state_dim * inner), BF16),
             pltpu.VMEM((chunks, tokens, inner), BF16),
             pltpu.VMEM((chunks, half, 2 * inner), BF16),
             pltpu.VMEM((half, 2 * inner), F32),
             pltpu.VMEM((half, 2 * p_dim), F32),
+            pltpu.VMEM((half, 2 * state_dim * inner), F32),
+            pltpu.VMEM((half, 2 * state_dim * inner), F32),
             pltpu.VMEM((chunks, half, 2 * p_dim), F32),
             pltpu.VMEM(p_half, F32),
             pltpu.VMEM(p_half, F32),
@@ -520,10 +527,7 @@
             pltpu.VMEM(y_half, BF16),
             pltpu.VMEM(y_half, BF16),
             pltpu.VMEM(y_half, BF16),
-            pltpu.VMEM((chunks, tokens, d_model), BF16),
             dma((6,)),
-            dma((1,)),
-            dma((1 + steps, chunks)),
             dma((chunks, 6)),
             dma((chunks, 6)),
             dma((chunks, 6)),
@@ -534,15 +538,19 @@
         y, h_new, conv_new = pl.pallas_call(
             layer_kernel,
             out_shape=(
-                jax.ShapeDtypeStruct(x_steps.shape, BF16),
-                jax.ShapeDtypeStruct(h_flat.shape, F32),
-                jax.ShapeDtypeStruct(conv_t.shape, BF16),
+                pltpu.VMEM(x_steps.shape, BF16),
+                pltpu.VMEM(h_flat.shape, F32),
+                pltpu.VMEM(conv_t.shape, BF16),
             ),
-            in_specs=[any_spec] * 7 + [vmem_spec] * 8,
-            out_specs=(any_spec, any_spec, vmem_spec),
+            in_specs=[any_spec] * 6 + [vmem_spec] * 16,
+            out_specs=(vmem_spec,) * 3,
             scratch_shapes=scratch,
-            compiler_params=pltpu.CompilerParams(collective_id=0, has_side_effects=True, vmem_limit_bytes=60 * 1024 * 1024),
-        )(x_steps, h_flat, ids, w_gate, w_up, w_down.reshape(experts * f_loc, d_model), w_out, conv_t, w_in2, vec, chan, w_xp.T, w_dt, a_log.T, w_router.T)
+            compiler_params=pltpu.CompilerParams(collective_id=0, has_side_effects=True, vmem_limit_bytes=52 * 1024 * 1024),
+        )(
+            x_steps, h_flat, w_gate, w_up, w_down.reshape(experts * f_loc, d_model), w_out,
+            jnp.transpose(expert_ids, (0, 2, 1)), conv_t, w_in.reshape(2 * d_model, inner), g_in, g_ff, conv_w.T, conv_b, b_dt, d_skip,
+            g_dt, g_b, g_c, w_xp.T, w_dt, a_log.T, w_router.T,
+        )
         h_new = jnp.swapaxes(h_new.reshape(batch, state_dim, inner), 1, 2)
         return y, jnp.transpose(conv_new, (1, 2, 0)), h_new
 

time: 113 us -> 89 us (0.79)
  local copies, waits for them, and re-layouts: 17.4 us -> 4.08 us
  Pallas kernels: 92.1 us -> 84.2 us
  other arithmetic: 2.6 us -> 0 us
    pallas_call x1, Pallas kernels: 92.1 us -> 84.2 us  [layer_steps(): pl.pallas_call(layer_kernel, out_shape=(pltpu.VMEM(x_steps.shape, BF16),...]
    concatenate x2 -> x0, local copies, waits for them, and re-layouts: 5.36 us -> none  [the longest x1 4.1 us: layer_steps(): jnp.concatenate([gains, gains])]
    unnamed x7 -> x3, local copies, waits for them, and re-layouts: 9.37 us -> 4.08 us
    another operation x2 -> x0, local copies, waits for them, and re-layouts: 1.36 us -> none  [layer_steps(): vec = jnp.stack([g_in, g_ff]).astype(F32)]
    another operation x2 -> x0, other arithmetic: 1.32 us -> none  [layer_steps(): jnp.stack([conv_b.astype(F32), b_dt.astype(F32), d_skip, jnp.concatenate(...]
    broadcast_in_dim x1 -> x0, local copies, waits for them, and re-layouts: 1.3 us -> none  [layer_steps(): ids = jnp.broadcast_to(expert_ids, (steps, batch, inner))]
    convert_element_type x2 -> x0, other arithmetic: 1.28 us -> none  [the longest x1 0.68 us: layer_steps(): conv_w.T.astype(F32)]
where the time goes in v2:
time: 89 us; the launch traced here: 88.9 us
  Pallas kernels  84.2 us (95%)
  local copies, waits for them, and re-layouts  4.08 us (5%)
    pallas_call x1, Pallas kernels, layer_steps(): pl.pallas_call(layer_kernel, out_shape=(pltpu.VMEM(x_steps.shape, BF16),...  84.2 us
    unnamed x3, local copies, waits for them, and re-layouts  4.08 us

profile of v2, /device:TPU:113, one launch (start us, length us, event | category | flops | bytes accessed | tf_op | source)
XLA Modules:
  0.0 88.9 jit_solution(14753481282679866782)
XLA Ops:
  0.6 84.2 %shard_map.229 = (bf16[4,512,512]{2,1,0:T(8,128)(2,1)S(1)}, f32[8192,128]{1,0:T(8,128)S(1)}, bf16[3,512,128]{2,1,0:T(8,128)(2,1)S(1)}) custom-call(bf16[4,512,512]{2,1,0:T(8,128)(2,1)} %x_hbm.1, f32[8192,128]{1,0:T(8,128)} %bitcast.17, bf16[16,512,256]{2,1,0:T(8,128)(2,1)} %wg_hbm.1, bf16[16,512,256]{2,1,0:T(8,128)(2,1)} %wu_hbm.1, ...), custom_call_target="tpu_custom_call" | custom-call | tf_op jit(solution)/shard_map/pallas_call | solution.py:538
  84.9 1.3 %copy.28 = bf16[4,512,512]{2,1,0:T(8,128)(2,1)} copy(bf16[4,512,512]{2,1,0:T(8,128)(2,1)S(1)} %get-tuple-element.9) | data formatting | bytes 4194304
  86.2 0.7 copy.29
  86.9 2.0 %copy.30 = f32[512,128,16]{1,2,0:T(8,128)} copy(f32[512,128,16]{1,2,0:T(8,128)S(1)} %bitcast.15) | data formatting | bytes 8388608

commit v3 on v2

--- a/solution.py
+++ b/solution.py
@@ -42,7 +42,7 @@
     g_dt_ref, g_b_ref, g_c_ref, w_xp_ref, w_dt_ref, a_log_ref, w_router_ref,
     y_ref, h_ref, conv_out_ref,
     xbuf, hbuf, idbuf, wg, wu, wd, w_in2, w_tmp, vec_ref, chan_ref, w_xp2, w_dt2, a2, spread,
-    zbuf, xcbuf, dbuf, pnbuf, bbuf, cbuf,
+    zbuf, xcbuf, dbuf, pnbuf, cbuf,
     p_part, p_r0, p_s1, p_r1, p_s2, p_r2, p_sum,
     yg_all, wo_all, ubuf, mbuf, qbuf, acc, prob,
     y_part, y_r0, y_s1, y_r1, y_s2, y_r2,
@@ -93,8 +93,7 @@
 
     def yg_block(ch):
         def block(c, x):
-            col = pl.ds(pl.multiple_of((c * 4 + x) * inner, inner), inner)
-            return yg_all, lambda lo, n: (ch, pl.ds(lo, n), col), tokens
+            return yg_all, lambda lo, n: (ch, c * 4 + x, pl.ds(lo, n)), tokens
         return block
 
     def ag_copies(block, k):
@@ -281,19 +280,16 @@
         parts = [jnp.where(is_c, v, 0.0) for v in (first, second, third)]
         split = parts[0] + pltpu.roll(parts[1], state_dim, 1) + pltpu.roll(parts[2], 2 * state_dim, 1)
         cbuf[...] = mm(split.astype(BF16), spread[...])
-        for k in range(2 * state_dim):
-            at = (k // state_dim) * p_dim + dt_rank + k % state_dim
-            bbuf[:, k * inner:(k + 1) * inner] = jnp.broadcast_to(pn[:, at:at + 1], (half_rows, inner))
         pre = mm(pn.astype(BF16), w_dt2[...])
         bias = chan_ref[5:6, :]
         pre = pre + jnp.concatenate([bias, bias], axis=1)
         dbuf[...] = jnp.maximum(pre, 0.0) + jnp.log1p(jnp.exp(-jnp.abs(pre)))
-        my_col = pl.ds(pl.multiple_of((core * 4 + chip) * inner, inner), inner)
+        mine = core * 4 + chip
         tile = 16
 
         def tile_body(bt, carry):
             r0 = pl.multiple_of(bt * tile, tile)
-            d, dx, y, ats = [], [], [], []
+            d, dx, y, ats, pns = [], [], [], [], []
             for s in range(steps):
                 at = pl.ds(pl.multiple_of((s % 2) * rows + r0, tile), tile)
                 cols = slice((s // 2) * inner, (s // 2 + 1) * inner)
@@ -303,19 +299,21 @@
                 dx.append(ds_ * xc)
                 y.append(chan_ref[6:7, :] * xc)
                 ats.append(at)
+                pns.append(pnbuf[at, :])
             for n in range(state_dim):
                 where = pl.ds((ch * rows + r0) * state_dim + n, tile, stride=state_dim)
                 h = hbuf[where, :]
                 a_n = a2[n:n + 1, :]
                 for s in range(steps):
                     k = (s // 2) * state_dim + n
-                    h = jnp.exp2(d[s] * a_n) * h + dx[s] * bbuf[ats[s], k * inner:(k + 1) * inner]
+                    kb = (s // 2) * p_dim + dt_rank + n
+                    h = jnp.exp2(d[s] * a_n) * h + dx[s] * pns[s][:, kb:kb + 1]
                     y[s] = y[s] + h * cbuf[ats[s], k * inner:(k + 1) * inner]
                 h_ref[where, :] = h
             for s in range(steps):
                 at = pl.ds(pl.multiple_of(s * rows + r0, tile), tile)
                 z = zbuf[ch, at, :].astype(F32)
-                yg_all[ch, at, my_col] = (y[s] * silu(z)).astype(BF16)
+                yg_all[ch, mine, at, :] = (y[s] * silu(z)).astype(BF16)
             return carry
 
         lax.fori_loop(0, rows // tile, tile_body, 0)
@@ -323,7 +321,7 @@
 
     def stage_mid(ch):
         ag_done(yg_block(ch), ch)
-        mix = mm(yg_all[ch], wo_all[...])
+        mix = mm(jnp.concatenate([yg_all[ch, k] for k in range(yg_all.shape[1])], axis=1), wo_all[...])
         xf = xbuf[:, chunk_rows(ch), :].reshape(tokens, d_model).astype(F32)
         u = (xf + mix).astype(BF16)
         ubuf[ch] = u
@@ -399,16 +397,14 @@
 
     def first_body(t):
         stage_in(t)
-        when_chunk(t - 2, p_one)
+        when_chunk(t - 3, p_one)
 
     loop(chunks, first_body)
-    p_one(chunks - 2)
-    p_one(chunks - 1)
-    for ch in range(4):
+    for ch in range(chunks - 3, chunks):
+        p_one(ch)
+    for ch in range(chunks):
         p_two(ch)
     ag_relay(wo_block, chunks)
-    for ch in range(4, chunks):
-        p_two(ch)
     for ch in range(3):
         p_three(ch)
     h_in.wait()
@@ -417,7 +413,7 @@
         stage_ssm(t)
         when_chunk(t + 3, p_three)
         when_chunk(t - 4, lambda ch: ag_relay(yg_block(ch), ch))
-        when_chunk(t - 6, lambda ch: ag_far(yg_block(ch), ch))
+        when_chunk(t - 7, lambda ch: ag_far(yg_block(ch), ch))
 
     loop(chunks, ssm_body)
     ag_far(wo_block, chunks)
@@ -434,7 +430,7 @@
                 when_chunk(t + 4, lambda ch: ag_relay(yg_block(ch), ch))
                 when_chunk(t - 4, y_three)
             elif g == 1:
-                when_chunk(t + 2, lambda ch: ag_far(yg_block(ch), ch))
+                when_chunk(t + 1, lambda ch: ag_far(yg_block(ch), ch))
                 when_chunk(t - 1, y_one)
             elif g == 2:
                 when_chunk(t - 2, y_two)
@@ -506,7 +502,6 @@
             pltpu.VMEM((half, 2 * inner), F32),
             pltpu.VMEM((half, 2 * p_dim), F32),
             pltpu.VMEM((half, 2 * state_dim * inner), F32),
-            pltpu.VMEM((half, 2 * state_dim * inner), F32),
             pltpu.VMEM((chunks, half, 2 * p_dim), F32),
             pltpu.VMEM(p_half, F32),
             pltpu.VMEM(p_half, F32),
@@ -514,7 +509,7 @@
             pltpu.VMEM(p_half, F32),
             pltpu.VMEM(p_half, F32),
             pltpu.VMEM((chunks, half, 2 * p_dim), F32),
-            pltpu.VMEM((chunks, tokens, group_inner), BF16),
+            pltpu.VMEM((chunks, group_inner // inner, tokens, inner), BF16),
             pltpu.VMEM((group_inner, d_model), BF16),
             pltpu.VMEM((chunks, tokens, d_model), BF16),
             pltpu.VMEM((tokens, d_model), BF16),

time: 89 us -> 89 us (level)
  no operation moved by 1% of the time
where the time goes in v3:
time: 89 us; the launch traced here: 88.9 us
  Pallas kernels  84.2 us (95%)
  local copies, waits for them, and re-layouts  4.08 us (5%)
    pallas_call x1, Pallas kernels, layer_steps(): pl.pallas_call(layer_kernel, out_shape=(pltpu.VMEM(x_steps.shape, BF16),...  84.2 us
    unnamed x3, local copies, waits for them, and re-layouts  4.08 us

profile of v3, /device:TPU:113, one launch (start us, length us, event | category | flops | bytes accessed | tf_op | source)
XLA Modules:
  0.0 88.9 jit_solution(10943575051556623084)
XLA Ops:
  0.6 84.2 %shard_map.229 = (bf16[4,512,512]{2,1,0:T(8,128)(2,1)S(1)}, f32[8192,128]{1,0:T(8,128)S(1)}, bf16[3,512,128]{2,1,0:T(8,128)(2,1)S(1)}) custom-call(bf16[4,512,512]{2,1,0:T(8,128)(2,1)} %x_hbm.1, f32[8192,128]{1,0:T(8,128)} %bitcast.17, bf16[16,512,256]{2,1,0:T(8,128)(2,1)} %wg_hbm.1, bf16[16,512,256]{2,1,0:T(8,128)(2,1)} %wu_hbm.1, ...), custom_call_target="tpu_custom_call" | custom-call | tf_op jit(solution)/shard_map/pallas_call | solution.py:533
  84.8 1.3 %copy.28 = bf16[4,512,512]{2,1,0:T(8,128)(2,1)} copy(bf16[4,512,512]{2,1,0:T(8,128)(2,1)S(1)} %get-tuple-element.9) | data formatting | bytes 4194304
  86.1 0.7 copy.29
  86.9 2.0 %copy.30 = f32[512,128,16]{1,2,0:T(8,128)} copy(f32[512,128,16]{1,2,0:T(8,128)S(1)} %bitcast.15) | data formatting | bytes 8388608

commit v4 on v3

--- a/solution.py
+++ b/solution.py
@@ -80,83 +80,71 @@
     w_ins = [pltpu.make_async_copy(src, dst, in_sem.at[2 + i]) for i, (src, dst) in enumerate(((wg_hbm, wg), (wu_hbm, wu), (wd_hbm, wd)))]
     my_rows = pl.ds(pl.multiple_of((core * 4 + chip) * inner, inner), inner)
     wo_in = pltpu.make_async_copy(w_out_hbm, wo_all.at[my_rows, :], in_sem.at[5])
-    x_in.start()
-    wo_in.start()
-
     barrier = pltpu.get_barrier_semaphore()
     for peer in (mate, peer_a, peer_b):
         pl.semaphore_signal(barrier, inc=1, device_id=peer, device_id_type=pl.DeviceIdType.MESH)
-    pl.semaphore_wait(barrier, 3)
+    x_in.start()
+    wo_in.start()
+    h_in.start()
 
     def wo_block(c, x):
-        return wo_all, lambda lo, n: (pl.ds(pl.multiple_of((c * 4 + x) * inner + lo, n), n), slice(None)), inner
+        return wo_all, lambda lo, n, blocks: (pl.ds(pl.multiple_of((c * 4 + x) * inner + lo, n), n * blocks), slice(None)), inner
 
     def yg_block(ch):
         def block(c, x):
-            return yg_all, lambda lo, n: (ch, c * 4 + x, pl.ds(lo, n)), tokens
+            return yg_all, lambda lo, n, blocks: (ch, pl.ds(c * 4 + x, blocks), pl.ds(lo, n)), tokens
         return block
 
     def ag_copies(block, k):
-        def cut(c, x, part=None):
+        def cut(c, x, part=None, blocks=1):
             ref, index, n = block(c, x)
             if part is None:
-                return ref.at[index(0, n)]
-            return ref.at[index(part * (n // 2), n // 2)]
-
-        def make(idx, src, peer, part=None):
-            return copy_to(cut(core, src, part), cut(core, src, part), g_send.at[k, idx], g_recv.at[k, idx], peer)
-
-        def take(idx, c, src, part=None):
-            return copy_to(cut(c, src, part), cut(c, src, part), g_send.at[k, idx], g_recv.at[k, idx], mate)
-
-        sends = Lazy(
-            own_a=lambda: make(0, chip, peer_a), own_b=lambda: make(1, chip, peer_b),
-            fwd_b=lambda: make(2, chip_a, peer_b, 0), fwd_a=lambda: make(3, chip_b, peer_a, 1),
-            m_own=lambda: make(4, chip, mate), m_a=lambda: make(5, chip_a, mate),
-            m_b=lambda: make(6, chip_b, mate), m_far=lambda: make(7, chip_far, mate),
+                return ref.at[index(0, n, blocks)]
+            return ref.at[index(part * (n // 2), n // 2, 1)]
+
+        def make(idx, c, src, peer, part=None, blocks=1):
+            ref = cut(c, src, part, blocks)
+            return copy_to(ref, ref, g_send.at[k], g_recv.at[k, idx], peer)
+
+        return Lazy(
+            own_a=lambda: make(0, core, chip, peer_a), own_b=lambda: make(1, core, chip, peer_b),
+            fwd_b=lambda: make(2, core, chip_a, peer_b, 0), fwd_a=lambda: make(2, core, chip_b, peer_a, 1),
+            m_own=lambda: make(3, core, chip, mate), m_a=lambda: make(3, core, chip_a, mate),
+            m_b=lambda: make(3, core, chip_b, mate), m_far=lambda: make(3, core, chip_far, mate),
+            got_a=lambda: make(0, core, chip_a, mate), got_b=lambda: make(1, core, chip_b, mate),
+            got_far=lambda: make(2, core, chip_far, mate), got_mate=lambda: make(3, other, 0, mate, blocks=4),
+            sent=lambda: make(3, 0, 0, mate, blocks=7),
         )
-        recvs = Lazy(
-            a=lambda: take(0, core, chip_a), b=lambda: take(1, core, chip_b),
-            far0=lambda: take(2, core, chip_far, 0), far1=lambda: take(3, core, chip_far, 1),
-            m_own=lambda: take(4, other, chip), m_a=lambda: take(5, other, chip_a),
-            m_b=lambda: take(6, other, chip_b), m_far=lambda: take(7, other, chip_far),
-        )
-        return sends, recvs
 
     def wo_first():
-        for idx, peer in ((0, peer_a), (1, peer_b), (4, mate)):
-            copy_to(w_out_hbm, wo_all.at[my_rows, :], g_send.at[chunks, idx], g_recv.at[chunks, idx], peer).start()
+        for idx, peer in ((0, peer_a), (1, peer_b), (3, mate)):
+            copy_to(w_out_hbm, wo_all.at[my_rows, :], g_send.at[chunks], g_recv.at[chunks, idx], peer).start()
 
     def ag_first(block, k):
-        s, _ = ag_copies(block, k)
-        s["own_a"].start()
-        s["own_b"].start()
-        s["m_own"].start()
+        cs = ag_copies(block, k)
+        cs["own_a"].start()
+        cs["own_b"].start()
+        cs["m_own"].start()
 
     def ag_relay(block, k):
-        s, r = ag_copies(block, k)
-        r["a"].wait_recv()
-        s["fwd_b"].start()
-        s["m_a"].start()
-        r["b"].wait_recv()
-        s["fwd_a"].start()
-        s["m_b"].start()
+        cs = ag_copies(block, k)
+        cs["got_a"].wait_recv()
+        cs["fwd_b"].start()
+        cs["got_b"].wait_recv()
+        cs["fwd_a"].start()
+        cs["m_a"].start()
+        cs["m_b"].start()
 
     def ag_far(block, k):
-        s, r = ag_copies(block, k)
-        r["far0"].wait_recv()
-        r["far1"].wait_recv()
-        s["m_far"].start()
+        cs = ag_copies(block, k)
+        cs["got_far"].wait_recv()
+        cs["m_far"].start()
 
     def ag_done(block, k):
-        _, r = ag_copies(block, k)
-        for name in ("m_own", "m_a", "m_b", "m_far"):
-            r[name].wait_recv()
+        ag_copies(block, k)["got_mate"].wait_recv()
 
     def ag_drain(block, k):
-        s, _ = ag_copies(block, k)
-        for name in ("own_a", "own_b", "fwd_b", "fwd_a", "m_own", "m_a", "m_b", "m_far"):
-            s[name].wait_send()
+        ag_copies(block, k)["sent"].wait_send()
 
     def ar_copies(part, r0, s1, r1, s2, r2, total_keep, total_give, send, recv, ch, n):
         q = n // 4
@@ -165,14 +153,16 @@
         lo, hi = pl.ds(0, q), pl.ds(q, q)
 
         def make(idx, src, dst, peer):
-            return copy_to(src, dst, send.at[ch, idx], recv.at[ch, idx], peer)
+            return copy_to(src, dst, send.at[ch], recv.at[ch, idx], peer)
 
         return Lazy(
             swap=lambda: make(0, part.at[ch, give], r0.at[ch], mate),
-            a1=lambda: make(1, s1.at[ch, lo], r1.at[ch, lo], peer_a), b1=lambda: make(2, s1.at[ch, hi], r1.at[ch, hi], peer_b),
-            a2=lambda: make(3, s2.at[ch, lo], r2.at[ch, lo], peer_b), b2=lambda: make(4, s2.at[ch, hi], r2.at[ch, hi], peer_a),
-            out=lambda: make(5, total_keep(), total_keep(), mate),
-            back=lambda: make(5, total_give(), total_give(), mate),
+            a1=lambda: make(1, s1.at[ch, lo], r1.at[ch, lo], peer_a), b1=lambda: make(1, s1.at[ch, hi], r1.at[ch, hi], peer_b),
+            a2=lambda: make(2, s2.at[ch, lo], r2.at[ch, lo], peer_b), b2=lambda: make(2, s2.at[ch, hi], r2.at[ch, hi], peer_a),
+            out=lambda: make(3, total_keep(), total_keep(), mate),
+            got_1=lambda: make(1, s1.at[ch], r1.at[ch], mate), got_2=lambda: make(2, s2.at[ch], r2.at[ch], mate),
+            back=lambda: make(3, total_give(), total_give(), mate),
+            sent=lambda: make(0, part.at[pl.ds(0, 2)], part.at[pl.ds(0, 2)], mate),
         ), keep
 
     def p_ar(ch):
@@ -192,8 +182,7 @@
         cs["b1"].start()
 
     def ar_two(cs, s1, r1, s2, ch):
-        cs["a1"].wait_recv()
-        cs["b1"].wait_recv()
+        cs["got_1"].wait_recv()
         s2[ch] = (s1[ch].astype(F32) + r1[ch].astype(F32)).astype(s2.dtype)
         cs["a2"].start()
         cs["b2"].start()
@@ -208,8 +197,7 @@
 
     def p_three(ch):
         cs, keep = p_ar(ch)
-        cs["a2"].wait_recv()
-        cs["b2"].wait_recv()
+        cs["got_2"].wait_recv()
         p_sum[ch, keep] = p_s2[ch] + p_r2[ch]
         cs["out"].start()
 
@@ -223,8 +211,7 @@
 
     def y_three(ch):
         cs, keep = y_ar(ch)
-        cs["a2"].wait_recv()
-        cs["b2"].wait_recv()
+        cs["got_2"].wait_recv()
         moe_sum = y_s2[ch].astype(F32) + y_r2[ch].astype(F32)
         y_new = (ubuf[ch, keep].astype(F32) + moe_sum).astype(BF16)
         y_ref[pl.ds(core * (steps // 2), steps // 2), chunk_rows(ch), :] = y_new.reshape(steps // 2, rows, d_model)
@@ -366,9 +353,6 @@
             return carry
         lax.fori_loop(0, n, step, 0)
 
-    wo_first()
-    for cp in (h_in, *w_ins):
-        cp.start()
     w_xp2[...] = jnp.zeros_like(w_xp2)
     w_dt2[...] = jnp.zeros_like(w_dt2)
     for k in range(2):
@@ -393,6 +377,10 @@
         spread[:, k * inner:(k + 1) * inner] = jnp.where(hit, 1.0, 0.0).astype(BF16)
     for s in range(steps):
         idbuf[s] = jnp.broadcast_to(ids_ref[s].astype(F32), (inner, batch)).T.astype(jnp.int32)
+    pl.semaphore_wait(barrier, 3)
+    wo_first()
+    for cp in w_ins:
+        cp.start()
     x_in.wait()
 
     def first_body(t):
@@ -404,16 +392,16 @@
         p_one(ch)
     for ch in range(chunks):
         p_two(ch)
-    ag_relay(wo_block, chunks)
     for ch in range(3):
         p_three(ch)
+    ag_relay(wo_block, chunks)
     h_in.wait()
 
     def ssm_body(t):
         stage_ssm(t)
         when_chunk(t + 3, p_three)
-        when_chunk(t - 4, lambda ch: ag_relay(yg_block(ch), ch))
-        when_chunk(t - 7, lambda ch: ag_far(yg_block(ch), ch))
+        when_chunk(t - 3, lambda ch: ag_relay(yg_block(ch), ch))
+        when_chunk(t - 6, lambda ch: ag_far(yg_block(ch), ch))
 
     loop(chunks, ssm_body)
     ag_far(wo_block, chunks)
@@ -427,20 +415,19 @@
         for g in range(experts // GROUP):
             stage_experts(t, g)
             if g == 0:
-                when_chunk(t + 4, lambda ch: ag_relay(yg_block(ch), ch))
-                when_chunk(t - 4, y_three)
+                when_chunk(t + 5, lambda ch: ag_relay(yg_block(ch), ch))
+                when_chunk(t - 1, y_one)
             elif g == 1:
-                when_chunk(t + 1, lambda ch: ag_far(yg_block(ch), ch))
-                when_chunk(t - 1, y_one)
+                when_chunk(t + 2, lambda ch: ag_far(yg_block(ch), ch))
+                when_chunk(t - 2, y_two)
             elif g == 2:
-                when_chunk(t - 2, y_two)
+                when_chunk(t - 3, y_three)
 
     loop(chunks, moe_body)
     last = chunks - 1
-    y_three(last - 3)
     y_two(last - 1)
+    y_one(last)
     y_three(last - 2)
-    y_one(last)
     y_three(last - 1)
     y_two(last)
     y_three(last)
@@ -449,8 +436,7 @@
         y_four(ch)
         ag_drain(yg_block(ch), ch)
         for cs, _ in (p_ar(ch), y_ar(ch)):
-            for name in ("swap", "a1", "b1", "a2", "b2", "out"):
-                cs[name].wait_send()
+            cs["sent"].wait_send()
 
     loop(chunks, drain)
     ag_drain(wo_block, chunks)
@@ -523,12 +509,12 @@
             pltpu.VMEM(y_half, BF16),
             pltpu.VMEM(y_half, BF16),
             dma((6,)),
-            dma((chunks, 6)),
-            dma((chunks, 6)),
-            dma((chunks, 6)),
-            dma((chunks, 6)),
-            dma((chunks + 1, 8)),
-            dma((chunks + 1, 8)),
+            dma((chunks,)),
+            dma((chunks, 4)),
+            dma((chunks,)),
+            dma((chunks, 4)),
+            dma((chunks + 1,)),
+            dma((chunks + 1, 4)),
         ]
         y, h_new, conv_new = pl.pallas_call(
             layer_kernel,

time: 89 us -> 85.2 us (0.957)
  Pallas kernels: 84.2 us -> 80.3 us
    pallas_call x1, Pallas kernels: 84.2 us -> 80.3 us  [layer_steps(): pl.pallas_call(layer_kernel, out_shape=(pltpu.VMEM(x_steps.shape, BF16),...]
where the time goes in v4:
time: 85.2 us; the launch traced here: 85.1 us
  Pallas kernels  80.3 us (94%)
  local copies, waits for them, and re-layouts  4.08 us (5%)
    pallas_call x1, Pallas kernels, layer_steps(): pl.pallas_call(layer_kernel, out_shape=(pltpu.VMEM(x_steps.shape, BF16),...  80.3 us
    unnamed x3, local copies, waits for them, and re-layouts  4.08 us

profile of v4, /device:TPU:113, one launch (start us, length us, event | category | flops | bytes accessed | tf_op | source)
XLA Modules:
  0.0 85.1 jit_solution(3789244720477198217)
XLA Ops:
  0.6 80.3 %shard_map.229 = (bf16[4,512,512]{2,1,0:T(8,128)(2,1)S(1)}, f32[8192,128]{1,0:T(8,128)S(1)}, bf16[3,512,128]{2,1,0:T(8,128)(2,1)S(1)}) custom-call(bf16[4,512,512]{2,1,0:T(8,128)(2,1)} %x_hbm.1, f32[8192,128]{1,0:T(8,128)} %bitcast.17, bf16[16,512,256]{2,1,0:T(8,128)(2,1)} %wg_hbm.1, bf16[16,512,256]{2,1,0:T(8,128)(2,1)} %wu_hbm.1, ...), custom_call_target="tpu_custom_call" | custom-call | tf_op jit(solution)/shard_map/pallas_call | solution.py:519
  81.0 1.3 %copy.28 = bf16[4,512,512]{2,1,0:T(8,128)(2,1)} copy(bf16[4,512,512]{2,1,0:T(8,128)(2,1)S(1)} %get-tuple-element.9) | data formatting | bytes 4194304
  82.3 0.7 copy.29
  83.1 2.0 %copy.30 = f32[512,128,16]{1,2,0:T(8,128)} copy(f32[512,128,16]{1,2,0:T(8,128)S(1)} %bitcast.15) | data formatting | bytes 8388608

commit v5 on v4

--- a/solution.py
+++ b/solution.py
@@ -42,7 +42,7 @@
     g_dt_ref, g_b_ref, g_c_ref, w_xp_ref, w_dt_ref, a_log_ref, w_router_ref,
     y_ref, h_ref, conv_out_ref,
     xbuf, hbuf, idbuf, wg, wu, wd, w_in2, w_tmp, vec_ref, chan_ref, w_xp2, w_dt2, a2, spread,
-    zbuf, xcbuf, dbuf, pnbuf, cbuf,
+    zbuf, xcbuf, yacc, pn_a, d_a, dx_a, pn_b, d_b, dx_b,
     p_part, p_r0, p_s1, p_r1, p_s2, p_r2, p_sum,
     yg_all, wo_all, ubuf, mbuf, qbuf, acc, prob,
     y_part, y_r0, y_s1, y_r1, y_s2, y_r2,
@@ -245,9 +245,7 @@
         cs, _ = p_ar(ch)
         cs["swap"].start()
 
-    def stage_ssm(ch):
-        cs, _ = p_ar(ch)
-        cs["back"].wait_recv()
+    def stage_norm(ch, pnbuf, dbuf, dxbuf):
         p = p_sum[ch]
         lane = lax.broadcasted_iota(jnp.int32, p.shape, 1)
         sq = p * p
@@ -259,52 +257,41 @@
                 mean = jnp.where(inside, total, mean)
         pn = p * lax.rsqrt(mean + EPSILON) * chan_ref[7:8, :]
         pnbuf[...] = pn
-        low = dt_rank + state_dim
-        is_c = (lane % p_dim) >= low
+        pre = mm(pn.astype(BF16), w_dt2[...])
+        bias = chan_ref[5:6, :]
+        pre = pre + jnp.concatenate([bias, bias], axis=1)
+        delta = jnp.maximum(pre, 0.0) + jnp.log1p(jnp.exp(-jnp.abs(pre)))
+        dbuf[...] = delta
+        dxbuf[...] = delta * xcbuf[ch].astype(F32)
+
+    def stage_ssm(ch, pnbuf, dbuf, dxbuf):
+        pn = pnbuf[...]
+        lane = lax.broadcasted_iota(jnp.int32, pn.shape, 1)
+        is_c = (lane % p_dim) >= dt_rank + state_dim
         first = pn.astype(BF16).astype(F32)
         second = (pn - first).astype(BF16).astype(F32)
         third = pn - first - second
         parts = [jnp.where(is_c, v, 0.0) for v in (first, second, third)]
-        split = parts[0] + pltpu.roll(parts[1], state_dim, 1) + pltpu.roll(parts[2], 2 * state_dim, 1)
-        cbuf[...] = mm(split.astype(BF16), spread[...])
-        pre = mm(pn.astype(BF16), w_dt2[...])
-        bias = chan_ref[5:6, :]
-        pre = pre + jnp.concatenate([bias, bias], axis=1)
-        dbuf[...] = jnp.maximum(pre, 0.0) + jnp.log1p(jnp.exp(-jnp.abs(pre)))
-        mine = core * 4 + chip
-        tile = 16
-
-        def tile_body(bt, carry):
-            r0 = pl.multiple_of(bt * tile, tile)
-            d, dx, y, ats, pns = [], [], [], [], []
+        split = (parts[0] + pltpu.roll(parts[1], state_dim, 1) + pltpu.roll(parts[2], 2 * state_dim, 1)).astype(BF16)
+        skip = chan_ref[6:7, :]
+
+        def at(s):
+            return slice((s % 2) * rows, (s % 2 + 1) * rows), slice((s // 2) * inner, (s // 2 + 1) * inner)
+
+        for s in range(steps):
+            yacc[s * rows:(s + 1) * rows, :] = skip * xcbuf[(ch, *at(s))].astype(F32)
+        for n in range(state_dim):
+            c_all = mm(split, spread[:, 2 * n * inner:2 * (n + 1) * inner])
+            b_all = [jnp.broadcast_to(pn[:, k:k + 1], (half_rows, inner)) for k in (dt_rank + n, p_dim + dt_rank + n)]
+            where = pl.ds(ch * rows * state_dim + n, rows, stride=state_dim)
+            h = hbuf[where, :]
+            a_n = a2[n:n + 1, :]
             for s in range(steps):
-                at = pl.ds(pl.multiple_of((s % 2) * rows + r0, tile), tile)
-                cols = slice((s // 2) * inner, (s // 2 + 1) * inner)
-                ds_ = dbuf[at, cols]
-                xc = xcbuf[ch, at, cols].astype(F32)
-                d.append(ds_)
-                dx.append(ds_ * xc)
-                y.append(chan_ref[6:7, :] * xc)
-                ats.append(at)
-                pns.append(pnbuf[at, :])
-            for n in range(state_dim):
-                where = pl.ds((ch * rows + r0) * state_dim + n, tile, stride=state_dim)
-                h = hbuf[where, :]
-                a_n = a2[n:n + 1, :]
-                for s in range(steps):
-                    k = (s // 2) * state_dim + n
-                    kb = (s // 2) * p_dim + dt_rank + n
-                    h = jnp.exp2(d[s] * a_n) * h + dx[s] * pns[s][:, kb:kb + 1]
-                    y[s] = y[s] + h * cbuf[ats[s], k * inner:(k + 1) * inner]
-                h_ref[where, :] = h
-            for s in range(steps):
-                at = pl.ds(pl.multiple_of(s * rows + r0, tile), tile)
-                z = zbuf[ch, at, :].astype(F32)
-                yg_all[ch, mine, at, :] = (y[s] * silu(z)).astype(BF16)
-            return carry
-
-        lax.fori_loop(0, rows // tile, tile_body, 0)
-        ag_first(yg_block(ch), ch)
+                r, c = at(s)
+                h = jnp.exp2(dbuf[r, c] * a_n) * h + dxbuf[r, c] * b_all[s // 2][r]
+                yacc[s * rows:(s + 1) * rows, :] += h * c_all[r, c]
+            h_ref[where, :] = h
+        yg_all[ch, core * 4 + chip] = (yacc[...] * silu(zbuf[ch].astype(F32))).astype(BF16)
 
     def stage_mid(ch):
         ag_done(yg_block(ch), ch)
@@ -372,7 +359,7 @@
     chan_ref[7:8, :] = jnp.concatenate(gains + gains, axis=1)
     row = lax.broadcasted_iota(jnp.int32, (2 * p_dim, inner), 0)
     for k in range(2 * state_dim):
-        at = (k // state_dim) * p_dim + dt_rank + state_dim + k % state_dim
+        at = (k % 2) * p_dim + dt_rank + state_dim + k // 2
         hit = (row == at) | (row == (at + state_dim) % (2 * p_dim)) | (row == (at + 2 * state_dim) % (2 * p_dim))
         spread[:, k * inner:(k + 1) * inner] = jnp.where(hit, 1.0, 0.0).astype(BF16)
     for s in range(steps):
@@ -397,13 +384,27 @@
     ag_relay(wo_block, chunks)
     h_in.wait()
 
-    def ssm_body(t):
-        stage_ssm(t)
+    even, odd = (pn_a, d_a, dx_a), (pn_b, d_b, dx_b)
+
+    def p_done(ch):
+        p_ar(ch)[0]["back"].wait_recv()
+
+    def ssm_tick(t, now, later):
+        when_chunk(t + 1, p_done)
+        stage_ssm(t, *now)
+        stage_norm(jnp.minimum(t + 1, chunks - 1), *later)
+        ag_first(yg_block(t), t)
         when_chunk(t + 3, p_three)
         when_chunk(t - 3, lambda ch: ag_relay(yg_block(ch), ch))
         when_chunk(t - 6, lambda ch: ag_far(yg_block(ch), ch))
 
-    loop(chunks, ssm_body)
+    def ssm_body(t):
+        ssm_tick(2 * t, even, odd)
+        ssm_tick(2 * t + 1, odd, even)
+
+    p_done(0)
+    stage_norm(0, *even)
+    loop(chunks // 2, ssm_body)
     ag_far(wo_block, chunks)
     wo_in.wait()
     for cp in w_ins:
@@ -485,9 +486,13 @@
             pltpu.VMEM((2 * p_dim, 2 * state_dim * inner), BF16),
             pltpu.VMEM((chunks, tokens, inner), BF16),
             pltpu.VMEM((chunks, half, 2 * inner), BF16),
+            pltpu.VMEM((tokens, inner), F32),
+            pltpu.VMEM((half, 2 * p_dim), F32),
+            pltpu.VMEM((half, 2 * inner), F32),
             pltpu.VMEM((half, 2 * inner), F32),
             pltpu.VMEM((half, 2 * p_dim), F32),
-            pltpu.VMEM((half, 2 * state_dim * inner), F32),
+            pltpu.VMEM((half, 2 * inner), F32),
+            pltpu.VMEM((half, 2 * inner), F32),
             pltpu.VMEM((chunks, half, 2 * p_dim), F32),
             pltpu.VMEM(p_half, F32),
             pltpu.VMEM(p_half, F32),

time: 85.2 us -> 83.5 us (0.980)
  Pallas kernels: 80.3 us -> 78.7 us
    pallas_call x1, Pallas kernels: 80.3 us -> 78.7 us  [layer_steps(): pl.pallas_call(layer_kernel, out_shape=(pltpu.VMEM(x_steps.shape, BF16),...]
where the time goes in v5:
time: 83.5 us; the launch traced here: 83.4 us
  Pallas kernels  78.7 us (94%)
  local copies, waits for them, and re-layouts  4.08 us (5%)
    pallas_call x1, Pallas kernels, layer_steps(): pl.pallas_call(layer_kernel, out_shape=(pltpu.VMEM(x_steps.shape, BF16),...  78.7 us
    unnamed x3, local copies, waits for them, and re-layouts  4.08 us

profile of v5, /device:TPU:113, one launch (start us, length us, event | category | flops | bytes accessed | tf_op | source)
XLA Modules:
  0.0 83.4 jit_solution(9183056688073430336)
XLA Ops:
  0.6 78.7 %shard_map.229 = (bf16[4,512,512]{2,1,0:T(8,128)(2,1)S(1)}, f32[8192,128]{1,0:T(8,128)S(1)}, bf16[3,512,128]{2,1,0:T(8,128)(2,1)S(1)}) custom-call(bf16[4,512,512]{2,1,0:T(8,128)(2,1)} %x_hbm.1, f32[8192,128]{1,0:T(8,128)} %bitcast.17, bf16[16,512,256]{2,1,0:T(8,128)(2,1)} %wg_hbm.1, bf16[16,512,256]{2,1,0:T(8,128)(2,1)} %wu_hbm.1, ...), custom_call_target="tpu_custom_call" | custom-call | tf_op jit(solution)/shard_map/pallas_call | solution.py:524
  79.3 1.3 %copy.28 = bf16[4,512,512]{2,1,0:T(8,128)(2,1)} copy(bf16[4,512,512]{2,1,0:T(8,128)(2,1)S(1)} %get-tuple-element.9) | data formatting | bytes 4194304
  80.6 0.7 copy.29
  81.4 2.0 %copy.30 = f32[512,128,16]{1,2,0:T(8,128)} copy(f32[512,128,16]{1,2,0:T(8,128)S(1)} %bitcast.15) | data formatting | bytes 8388608

commit v6 on v5

--- a/solution.py
+++ b/solution.py
@@ -44,7 +44,7 @@
     xbuf, hbuf, idbuf, wg, wu, wd, w_in2, w_tmp, vec_ref, chan_ref, w_xp2, w_dt2, a2, spread,
     zbuf, xcbuf, yacc, pn_a, d_a, dx_a, pn_b, d_b, dx_b,
     p_part, p_r0, p_s1, p_r1, p_s2, p_r2, p_sum,
-    yg_all, wo_all, ubuf, mbuf, qbuf, acc, prob,
+    yg_all, wo_all, ubuf, m_a, m_b, qbuf, acc, prob_a, prob_b,
     y_part, y_r0, y_s1, y_r1, y_s2, y_r2,
     in_sem, p_send, p_recv, y_send, y_recv, g_send, g_recv,
 ):
@@ -85,7 +85,6 @@
         pl.semaphore_signal(barrier, inc=1, device_id=peer, device_id_type=pl.DeviceIdType.MESH)
     x_in.start()
     wo_in.start()
-    h_in.start()
 
     def wo_block(c, x):
         return wo_all, lambda lo, n, blocks: (pl.ds(pl.multiple_of((c * 4 + x) * inner + lo, n), n * blocks), slice(None)), inner
@@ -293,17 +292,19 @@
             h_ref[where, :] = h
         yg_all[ch, core * 4 + chip] = (yacc[...] * silu(zbuf[ch].astype(F32))).astype(BF16)
 
-    def stage_mid(ch):
-        ag_done(yg_block(ch), ch)
+    def mid_one(ch):
         mix = mm(jnp.concatenate([yg_all[ch, k] for k in range(yg_all.shape[1])], axis=1), wo_all[...])
         xf = xbuf[:, chunk_rows(ch), :].reshape(tokens, d_model).astype(F32)
         u = (xf + mix).astype(BF16)
         ubuf[ch] = u
-        uf = u.astype(F32)
+
+    def mid_two(ch, mbuf):
+        uf = ubuf[ch].astype(F32)
         scale = lax.rsqrt(jnp.mean(uf * uf, axis=-1, keepdims=True) + EPSILON)
-        m = (uf * scale * vec_ref[1:2, :]).astype(BF16)
-        mbuf[...] = m
-        logits = nt_dot(m, w_router_ref[...])
+        mbuf[...] = (uf * scale * vec_ref[1:2, :]).astype(BF16)
+
+    def mid_three(ch, mbuf, prob):
+        logits = nt_dot(mbuf[...], w_router_ref[...])
         peak = jnp.max(logits, axis=-1, keepdims=True)
         ex = jnp.exp(logits - peak)
         ids = idbuf[:, chunk_rows(ch), 0:experts].reshape(tokens, experts)
@@ -311,7 +312,10 @@
         chosen = jnp.sum(jnp.where(hit, ex, 0.0), axis=-1, keepdims=True) / jnp.sum(ex, axis=-1, keepdims=True)
         prob[...] = jnp.broadcast_to(chosen, prob.shape)
 
-    def stage_experts(ch, g):
+    def mid_parts(ch, mbuf, prob):
+        return [lambda: mid_one(ch), lambda: mid_two(ch, mbuf), lambda: mid_three(ch, mbuf, prob)]
+
+    def stage_experts(ch, g, mbuf, prob, between=()):
         m = mbuf[...]
         ids = idbuf[:, chunk_rows(ch), :].reshape(tokens, inner)
         ids = jnp.concatenate([ids] * (f_loc // inner), axis=1)
@@ -319,6 +323,8 @@
             e = g * GROUP + j
             q = silu(mm(m, wg[e])) * mm(m, wu[e])
             qbuf[:, j * f_loc:(j + 1) * f_loc] = jnp.where(ids == e, q, 0.0).astype(BF16)
+            if j < len(between):
+                between[j]()
         part = mm(qbuf[...], wd[g * GROUP * f_loc:(g + 1) * GROUP * f_loc, :])
         if g == 0:
             acc[...] = part
@@ -328,8 +334,6 @@
             total = acc[...] + part
             weight = jnp.concatenate([prob[...]] * (d_model // inner), axis=1)
             y_part[ch] = (total * weight).astype(BF16)
-            cs, _ = y_ar(ch)
-            cs["swap"].start()
 
     def when_chunk(ch, fn):
         pl.when((ch >= 0) & (ch < chunks))(lambda: fn(ch))
@@ -365,8 +369,7 @@
     for s in range(steps):
         idbuf[s] = jnp.broadcast_to(ids_ref[s].astype(F32), (inner, batch)).T.astype(jnp.int32)
     pl.semaphore_wait(barrier, 3)
-    wo_first()
-    for cp in w_ins:
+    for cp in (h_in, *w_ins):
         cp.start()
     x_in.wait()
 
@@ -379,9 +382,9 @@
         p_one(ch)
     for ch in range(chunks):
         p_two(ch)
+    wo_first()
     for ch in range(3):
         p_three(ch)
-    ag_relay(wo_block, chunks)
     h_in.wait()
 
     even, odd = (pn_a, d_a, dx_a), (pn_b, d_b, dx_b)
@@ -395,6 +398,7 @@
         stage_norm(jnp.minimum(t + 1, chunks - 1), *later)
         ag_first(yg_block(t), t)
         when_chunk(t + 3, p_three)
+        pl.when(t == 3)(lambda: ag_relay(wo_block, chunks))
         when_chunk(t - 3, lambda ch: ag_relay(yg_block(ch), ch))
         when_chunk(t - 6, lambda ch: ag_far(yg_block(ch), ch))
 
@@ -411,20 +415,37 @@
         cp.wait()
     ag_done(wo_block, chunks)
 
-    def moe_body(t):
-        stage_mid(t)
-        for g in range(experts // GROUP):
-            stage_experts(t, g)
+    def got_yg(ch):
+        ag_done(yg_block(ch), ch)
+
+    def moe_tick(t, now, later):
+        for g in range(experts // GROUP - 1):
+            stage_experts(t, g, *now)
             if g == 0:
                 when_chunk(t + 5, lambda ch: ag_relay(yg_block(ch), ch))
                 when_chunk(t - 1, y_one)
             elif g == 1:
                 when_chunk(t + 2, lambda ch: ag_far(yg_block(ch), ch))
                 when_chunk(t - 2, y_two)
-            elif g == 2:
+            else:
                 when_chunk(t - 3, y_three)
-
-    loop(chunks, moe_body)
+        if later is not None:
+            got_yg(t + 1)
+        stage_experts(t, experts // GROUP - 1, *now, mid_parts(t + 1, *later) if later is not None else ())
+        y_ar(t)[0]["swap"].start()
+
+    even, odd = (m_a, prob_a), (m_b, prob_b)
+
+    def moe_body(i):
+        moe_tick(2 * i, even, odd)
+        moe_tick(2 * i + 1, odd, even)
+
+    got_yg(0)
+    for part in mid_parts(0, *even):
+        part()
+    loop(chunks // 2 - 1, moe_body)
+    moe_tick(chunks - 2, even, odd)
+    moe_tick(chunks - 1, odd, None)
     last = chunks - 1
     y_two(last - 1)
     y_one(last)
@@ -441,6 +462,15 @@
 
     loop(chunks, drain)
     ag_drain(wo_block, chunks)
+
+
+def store_kernel(y_in, h_in, conv_in, y_out, h_out, conv_out, sem):
+    pairs = ((h_in, h_out), (y_in, y_out), (conv_in, conv_out))
+    copies = [pltpu.make_async_copy(src, dst, sem.at[i]) for i, (src, dst) in enumerate(pairs)]
+    for cp in copies:
+        cp.start()
+    for cp in copies:
+        cp.wait()
 
 
 def solution(mesh):
@@ -504,8 +534,10 @@
             pltpu.VMEM((group_inner, d_model), BF16),
             pltpu.VMEM((chunks, tokens, d_model), BF16),
             pltpu.VMEM((tokens, d_model), BF16),
+            pltpu.VMEM((tokens, d_model), BF16),
             pltpu.VMEM((tokens, GROUP * f_loc), BF16),
             pltpu.VMEM((tokens, d_model), F32),
+            pltpu.VMEM((tokens, inner), F32),
             pltpu.VMEM((tokens, inner), F32),
             pltpu.VMEM((chunks, tokens, d_model), BF16),
             pltpu.VMEM(y_half, BF16),
@@ -531,12 +563,20 @@
             in_specs=[any_spec] * 6 + [vmem_spec] * 16,
             out_specs=(vmem_spec,) * 3,
             scratch_shapes=scratch,
-            compiler_params=pltpu.CompilerParams(collective_id=0, has_side_effects=True, vmem_limit_bytes=52 * 1024 * 1024),
+            compiler_params=pltpu.CompilerParams(collective_id=0, has_side_effects=True, vmem_limit_bytes=57 * 1024 * 1024),
         )(
             x_steps, h_flat, w_gate, w_up, w_down.reshape(experts * f_loc, d_model), w_out,
             jnp.transpose(expert_ids, (0, 2, 1)), conv_t, w_in.reshape(2 * d_model, inner), g_in, g_ff, conv_w.T, conv_b, b_dt, d_skip,
             g_dt, g_b, g_c, w_xp.T, w_dt, a_log.T, w_router.T,
         )
+        y, h_new, conv_new = pl.pallas_call(
+            store_kernel,
+            out_shape=[jax.ShapeDtypeStruct(v.shape, v.dtype) for v in (y, h_new, conv_new)],
+            in_specs=[vmem_spec] * 3,
+            out_specs=[any_spec] * 3,
+            scratch_shapes=[dma((3,))],
+            compiler_params=pltpu.CompilerParams(vmem_limit_bytes=1024 * 1024),
+        )(*(pltpu.with_memory_space_constraint(v, pltpu.VMEM) for v in (y, h_new, conv_new)))
         h_new = jnp.swapaxes(h_new.reshape(batch, state_dim, inner), 1, 2)
         return y, jnp.transpose(conv_new, (1, 2, 0)), h_new
 

time: 83.5 us -> 83.3 us (level)
  local copies, waits for them, and re-layouts: 4.08 us -> 0 us
  Pallas kernels: 78.7 us -> 82.4 us
    unnamed x3 -> x0, local copies, waits for them, and re-layouts: 4.08 us -> none
    pallas_call x0 -> x1, Pallas kernels: none -> 2.79 us  [layer_steps(): pl.pallas_call(store_kernel, out_shape=[jax.ShapeDtypeStruct(v.shape, v.d...]
    pallas_call x1, Pallas kernels: 78.7 us -> 79.6 us  [layer_steps(): pl.pallas_call(layer_kernel, out_shape=(pltpu.VMEM(x_steps.shape, BF16),...]
where the time goes in v6:
time: 83.3 us; the launch traced here: 83.2 us
  Pallas kernels  82.4 us (99%)
    pallas_call x1, Pallas kernels, layer_steps(): pl.pallas_call(layer_kernel, out_shape=(pltpu.VMEM(x_steps.shape, BF16),...  79.6 us
    pallas_call x1, Pallas kernels, layer_steps(): pl.pallas_call(store_kernel, out_shape=[jax.ShapeDtypeStruct(v.shape, v.d...  2.79 us

profile of v6, /device:TPU:113, one launch (start us, length us, event | category | flops | bytes accessed | tf_op | source)
XLA Modules:
  0.0 83.2 jit_solution(11838006672271420284)
XLA Ops:
  0.6 79.6 %shard_map.229 = (bf16[4,512,512]{2,1,0:T(8,128)(2,1)S(1)}, f32[8192,128]{1,0:T(8,128)S(1)}, bf16[3,512,128]{2,1,0:T(8,128)(2,1)S(1)}) custom-call(bf16[4,512,512]{2,1,0:T(8,128)(2,1)} %x_hbm.1, f32[8192,128]{1,0:T(8,128)} %bitcast.15, bf16[16,512,256]{2,1,0:T(8,128)(2,1)} %wg_hbm.1, bf16[16,512,256]{2,1,0:T(8,128)(2,1)} %wu_hbm.1, ...), custom_call_target="tpu_custom_call" | custom-call | tf_op jit(solution)/shard_map/pallas_call | solution.py:556
  80.2 2.8 %shard_map.230 = (bf16[4,512,512]{2,1,0:T(8,128)(2,1)}, f32[8192,128]{1,0:T(8,128)}, bf16[3,512,128]{2,1,0:T(8,128)(2,1)}) custom-call(bf16[4,512,512]{2,1,0:T(8,128)(2,1)S(1)} %get-tuple-element.9.y_in, f32[8192,128]{1,0:T(8,128)S(1)} %get-tuple-element.10.h_in, bf16[3,512,128]{2,1,0:T(8,128)(2,1)S(1)} %get-tuple-element.11.conv_in), custom_call_target="tpu_custom_call" | custom-call | tf_op jit(solution)/shard_map/pallas_call | solution.py:572

commit v7 on v6

--- a/solution.py
+++ b/solution.py
@@ -369,6 +369,7 @@
     for s in range(steps):
         idbuf[s] = jnp.broadcast_to(ids_ref[s].astype(F32), (inner, batch)).T.astype(jnp.int32)
     pl.semaphore_wait(barrier, 3)
+    wo_first()
     for cp in (h_in, *w_ins):
         cp.start()
     x_in.wait()
@@ -382,9 +383,9 @@
         p_one(ch)
     for ch in range(chunks):
         p_two(ch)
-    wo_first()
     for ch in range(3):
         p_three(ch)
+    ag_relay(wo_block, chunks)
     h_in.wait()
 
     even, odd = (pn_a, d_a, dx_a), (pn_b, d_b, dx_b)
@@ -398,7 +399,7 @@
         stage_norm(jnp.minimum(t + 1, chunks - 1), *later)
         ag_first(yg_block(t), t)
         when_chunk(t + 3, p_three)
-        pl.when(t == 3)(lambda: ag_relay(wo_block, chunks))
+        pl.when(t == 4)(lambda: ag_far(wo_block, chunks))
         when_chunk(t - 3, lambda ch: ag_relay(yg_block(ch), ch))
         when_chunk(t - 6, lambda ch: ag_far(yg_block(ch), ch))
 
@@ -409,7 +410,6 @@
     p_done(0)
     stage_norm(0, *even)
     loop(chunks // 2, ssm_body)
-    ag_far(wo_block, chunks)
     wo_in.wait()
     for cp in w_ins:
         cp.wait()
@@ -423,12 +423,12 @@
             stage_experts(t, g, *now)
             if g == 0:
                 when_chunk(t + 5, lambda ch: ag_relay(yg_block(ch), ch))
-                when_chunk(t - 1, y_one)
+                when_chunk(t - 4, y_three)
             elif g == 1:
                 when_chunk(t + 2, lambda ch: ag_far(yg_block(ch), ch))
+                when_chunk(t - 1, y_one)
+            else:
                 when_chunk(t - 2, y_two)
-            else:
-                when_chunk(t - 3, y_three)
         if later is not None:
             got_yg(t + 1)
         stage_experts(t, experts // GROUP - 1, *now, mid_parts(t + 1, *later) if later is not None else ())
@@ -447,11 +447,12 @@
     moe_tick(chunks - 2, even, odd)
     moe_tick(chunks - 1, odd, None)
     last = chunks - 1
+    y_three(last - 3)
+    y_one(last)
     y_two(last - 1)
-    y_one(last)
     y_three(last - 2)
+    y_two(last)
     y_three(last - 1)
-    y_two(last)
     y_three(last)
 
     def drain(ch):

time: 83.3 us -> 78.5 us (0.942)
  Pallas kernels: 82.4 us -> 77.5 us
    pallas_call x1, Pallas kernels: 79.6 us -> 74.8 us  [layer_steps(): pl.pallas_call(layer_kernel, out_shape=(pltpu.VMEM(x_steps.shape, BF16),...]
where the time goes in v7:
time: 78.5 us; the launch traced here: 78.4 us
  Pallas kernels  77.5 us (99%)
  between operations  0.81 us (1%)
    pallas_call x1, Pallas kernels, layer_steps(): pl.pallas_call(layer_kernel, out_shape=(pltpu.VMEM(x_steps.shape, BF16),...  74.8 us
    pallas_call x1, Pallas kernels, layer_steps(): pl.pallas_call(store_kernel, out_shape=[jax.ShapeDtypeStruct(v.shape, v.d...  2.79 us

profile of v7, /device:TPU:113, one launch (start us, length us, event | category | flops | bytes accessed | tf_op | source)
XLA Modules:
  0.0 78.4 jit_solution(17827016669878669796)
XLA Ops:
  0.6 74.8 %shard_map.229 = (bf16[4,512,512]{2,1,0:T(8,128)(2,1)S(1)}, f32[8192,128]{1,0:T(8,128)S(1)}, bf16[3,512,128]{2,1,0:T(8,128)(2,1)S(1)}) custom-call(bf16[4,512,512]{2,1,0:T(8,128)(2,1)} %x_hbm.1, f32[8192,128]{1,0:T(8,128)} %bitcast.15, bf16[16,512,256]{2,1,0:T(8,128)(2,1)} %wg_hbm.1, bf16[16,512,256]{2,1,0:T(8,128)(2,1)} %wu_hbm.1, ...), custom_call_target="tpu_custom_call" | custom-call | tf_op jit(solution)/shard_map/pallas_call | solution.py:557
  75.4 2.8 %shard_map.230 = (bf16[4,512,512]{2,1,0:T(8,128)(2,1)}, f32[8192,128]{1,0:T(8,128)}, bf16[3,512,128]{2,1,0:T(8,128)(2,1)}) custom-call(bf16[4,512,512]{2,1,0:T(8,128)(2,1)S(1)} %get-tuple-element.9.y_in, f32[8192,128]{1,0:T(8,128)S(1)} %get-tuple-element.10.h_in, bf16[3,512,128]{2,1,0:T(8,128)(2,1)S(1)} %get-tuple-element.11.conv_in), custom_call_target="tpu_custom_call" | custom-call | tf_op jit(solution)/shard_map/pallas_call | solution.py:573

commit v8 on v7

--- a/solution.py
+++ b/solution.py
@@ -37,18 +37,18 @@
 
 
 def layer_kernel(
-    x_hbm, h_hbm, wg_hbm, wu_hbm, wd_hbm, w_out_hbm,
+    x_ref, h_hbm, wg_hbm, wu_hbm, wd_hbm, w_out_hbm,
     ids_ref, conv_ref, w_in_ref, g_in_ref, g_ff_ref, conv_w_ref, conv_b_ref, b_dt_ref, d_skip_ref,
     g_dt_ref, g_b_ref, g_c_ref, w_xp_ref, w_dt_ref, a_log_ref, w_router_ref,
     y_ref, h_ref, conv_out_ref,
-    xbuf, hbuf, idbuf, wg, wu, wd, w_in2, w_tmp, vec_ref, chan_ref, w_xp2, w_dt2, a2, spread,
+    hbuf, idbuf, wg, wu, wd, w_in2, w_tmp, vec_ref, chan_ref, w_xp2, w_dt2, a2, spread,
     zbuf, xcbuf, yacc, pn_a, d_a, dx_a, pn_b, d_b, dx_b,
     p_part, p_r0, p_s1, p_r1, p_s2, p_r2, p_sum,
     yg_all, wo_all, ubuf, m_a, m_b, qbuf, acc, prob_a, prob_b,
     y_part, y_r0, y_s1, y_r1, y_s2, y_r2,
-    in_sem, p_send, p_recv, y_send, y_recv, g_send, g_recv,
+    in_sem, p_send, p_recv, y_send, y_recv, l_recv, g_send, g_recv,
 ):
-    steps, batch, d_model = x_hbm.shape
+    steps, batch, d_model = x_ref.shape
     state_dim, inner = a_log_ref.shape
     dt_rank = w_dt_ref.shape[0]
     p_dim = w_xp_ref.shape[0]
@@ -75,7 +75,6 @@
             src_ref=src, dst_ref=dst, send_sem=send_sem, recv_sem=recv_sem, device_id=peer, device_id_type=pl.DeviceIdType.MESH
         )
 
-    x_in = pltpu.make_async_copy(x_hbm, xbuf, in_sem.at[0])
     h_in = pltpu.make_async_copy(h_hbm, hbuf, in_sem.at[1])
     w_ins = [pltpu.make_async_copy(src, dst, in_sem.at[2 + i]) for i, (src, dst) in enumerate(((wg_hbm, wg), (wu_hbm, wu), (wd_hbm, wd)))]
     my_rows = pl.ds(pl.multiple_of((core * 4 + chip) * inner, inner), inner)
@@ -83,7 +82,6 @@
     barrier = pltpu.get_barrier_semaphore()
     for peer in (mate, peer_a, peer_b):
         pl.semaphore_signal(barrier, inc=1, device_id=peer, device_id_type=pl.DeviceIdType.MESH)
-    x_in.start()
     wo_in.start()
 
     def wo_block(c, x):
@@ -224,7 +222,7 @@
         return pl.ds(pl.multiple_of(ch * rows, rows), rows)
 
     def stage_in(ch):
-        xf = xbuf[:, chunk_rows(ch), :].reshape(tokens, d_model).astype(F32)
+        xf = x_ref[:, chunk_rows(ch), :].reshape(tokens, d_model).astype(F32)
         scale = lax.rsqrt(jnp.mean(xf * xf, axis=-1, keepdims=True) + EPSILON)
         norm = (xf * scale * vec_ref[0:1, :]).astype(BF16)
         proj = mm(norm, w_in2[...]).astype(BF16)
@@ -294,7 +292,7 @@
 
     def mid_one(ch):
         mix = mm(jnp.concatenate([yg_all[ch, k] for k in range(yg_all.shape[1])], axis=1), wo_all[...])
-        xf = xbuf[:, chunk_rows(ch), :].reshape(tokens, d_model).astype(F32)
+        xf = x_ref[:, chunk_rows(ch), :].reshape(tokens, d_model).astype(F32)
         u = (xf + mix).astype(BF16)
         ubuf[ch] = u
 
@@ -372,7 +370,6 @@
     wo_first()
     for cp in (h_in, *w_ins):
         cp.start()
-    x_in.wait()
 
     def first_body(t):
         stage_in(t)
@@ -393,19 +390,35 @@
     def p_done(ch):
         p_ar(ch)[0]["back"].wait_recv()
 
-    def ssm_tick(t, now, later):
+    gather_plan = (
+        [(ag_first, 0)],
+        [(ag_first, 1)],
+        [],
+        [(ag_relay, 0), (ag_first, 2)],
+        [(ag_first, 3), (ag_far, None)],
+        [(ag_relay, 1), (ag_first, 4)],
+        [(ag_first, 5), (ag_far, 0)],
+        [(ag_relay, 2)] + [(ag_first, ch) for ch in range(6, chunks)],
+    )
+
+    def ssm_tick(t, now, later, parity):
         when_chunk(t + 1, p_done)
         stage_ssm(t, *now)
         stage_norm(jnp.minimum(t + 1, chunks - 1), *later)
-        ag_first(yg_block(t), t)
         when_chunk(t + 3, p_three)
-        pl.when(t == 4)(lambda: ag_far(wo_block, chunks))
-        when_chunk(t - 3, lambda ch: ag_relay(yg_block(ch), ch))
-        when_chunk(t - 6, lambda ch: ag_far(yg_block(ch), ch))
+        for tick, events in enumerate(gather_plan):
+            if tick % 2 == parity and events:
+                def run(events=events):
+                    for fn, ch in events:
+                        if ch is None:
+                            fn(wo_block, chunks)
+                        else:
+                            fn(yg_block(ch), ch)
+                pl.when(t == tick)(run)
 
     def ssm_body(t):
-        ssm_tick(2 * t, even, odd)
-        ssm_tick(2 * t + 1, odd, even)
+        ssm_tick(2 * t, even, odd, 0)
+        ssm_tick(2 * t + 1, odd, even, 1)
 
     p_done(0)
     stage_norm(0, *even)
@@ -422,10 +435,12 @@
         for g in range(experts // GROUP - 1):
             stage_experts(t, g, *now)
             if g == 0:
-                when_chunk(t + 5, lambda ch: ag_relay(yg_block(ch), ch))
+                pl.when((t >= 1) & (2 * t + 2 < chunks))(lambda: ag_relay(yg_block(2 * t + 2), 2 * t + 2))
+                pl.when((t >= 1) & (t + 1 < chunks))(lambda: ag_far(yg_block(t + 1), t + 1))
                 when_chunk(t - 4, y_three)
             elif g == 1:
-                when_chunk(t + 2, lambda ch: ag_far(yg_block(ch), ch))
+                pl.when(t == 0)(lambda: ag_far(yg_block(1), 1))
+                pl.when(2 * t + 3 < chunks)(lambda: ag_relay(yg_block(2 * t + 3), 2 * t + 3))
                 when_chunk(t - 1, y_one)
             else:
                 when_chunk(t - 2, y_two)
@@ -447,13 +462,50 @@
     moe_tick(chunks - 2, even, odd)
     moe_tick(chunks - 1, odd, None)
     last = chunks - 1
+    quarter = tokens // 4
+    pieces = 2
+    piece = quarter // pieces
+
+    def last_copy(step, i, src, dst, peers):
+        for part, peer in enumerate(peers):
+            at = pl.ds(part * quarter + i * piece, piece)
+            yield copy_to(src.at[last, at], dst.at[last, at], y_send.at[last], l_recv.at[step, part, i], peer)
+
+    def last_one():
+        cs, keep = y_ar(last)
+        cs["swap"].wait_recv()
+        y_s1[last] = (y_part[last, keep].astype(F32) + y_r0[last].astype(F32)).astype(BF16)
+        for i in range(pieces):
+            for cp in last_copy(0, i, y_s1, y_r1, (peer_a, peer_b)):
+                cp.start()
+
+    def last_two():
+        for i in range(pieces):
+            for cp in last_copy(0, i, y_s1, y_r1, (peer_a, peer_b)):
+                cp.wait_recv()
+            for part in range(2):
+                at = pl.ds(part * quarter + i * piece, piece)
+                y_s2[last, at] = (y_s1[last, at].astype(F32) + y_r1[last, at].astype(F32)).astype(BF16)
+            for cp in last_copy(1, i, y_s2, y_r2, (peer_b, peer_a)):
+                cp.start()
+
+    def last_three():
+        for i in range(pieces):
+            for cp in last_copy(1, i, y_s2, y_r2, (peer_b, peer_a)):
+                cp.wait_recv()
+        cs, keep = y_ar(last)
+        moe_sum = y_s2[last].astype(F32) + y_r2[last].astype(F32)
+        y_new = (ubuf[last, keep].astype(F32) + moe_sum).astype(BF16)
+        y_ref[pl.ds(core * (steps // 2), steps // 2), chunk_rows(last), :] = y_new.reshape(steps // 2, rows, d_model)
+        cs["out"].start()
+
     y_three(last - 3)
-    y_one(last)
+    last_one()
     y_two(last - 1)
     y_three(last - 2)
-    y_two(last)
+    last_two()
     y_three(last - 1)
-    y_three(last)
+    last_three()
 
     def drain(ch):
         y_four(ch)
@@ -501,7 +553,6 @@
         y_half = (chunks, half, d_model)
         dma = pltpu.SemaphoreType.DMA
         scratch = [
-            pltpu.VMEM(x_steps.shape, BF16),
             pltpu.VMEM(h_flat.shape, F32),
             pltpu.VMEM((steps, batch, inner), jnp.int32),
             pltpu.VMEM(w_gate.shape, BF16),
@@ -551,6 +602,7 @@
             dma((chunks, 4)),
             dma((chunks,)),
             dma((chunks, 4)),
+            dma((2, 2, 2)),
             dma((chunks + 1,)),
             dma((chunks + 1, 4)),
         ]
@@ -561,7 +613,7 @@
                 pltpu.VMEM(h_flat.shape, F32),
                 pltpu.VMEM(conv_t.shape, BF16),
             ),
-            in_specs=[any_spec] * 6 + [vmem_spec] * 16,
+            in_specs=[vmem_spec] + [any_spec] * 5 + [vmem_spec] * 16,
             out_specs=(vmem_spec,) * 3,
             scratch_shapes=scratch,
             compiler_params=pltpu.CompilerParams(collective_id=0, has_side_effects=True, vmem_limit_bytes=57 * 1024 * 1024),

time: 78.5 us -> 78.1 us (level)
  no operation moved by 1% of the time
where the time goes in v8:
time: 78.1 us; the launch traced here: 78 us
  Pallas kernels  77.2 us (99%)
  between operations  0.81 us (1%)
    pallas_call x1, Pallas kernels, layer_steps(): pl.pallas_call(layer_kernel, out_shape=(pltpu.VMEM(x_steps.shape, BF16),...  74.4 us
    pallas_call x1, Pallas kernels, layer_steps(): pl.pallas_call(store_kernel, out_shape=[jax.ShapeDtypeStruct(v.shape, v.d...  2.79 us

profile of v8, /device:TPU:113, one launch (start us, length us, event | category | flops | bytes accessed | tf_op | source)
XLA Modules:
  0.0 78.0 jit_solution(7830518664300195905)
XLA Ops:
  0.6 74.4 %shard_map.229 = (bf16[4,512,512]{2,1,0:T(8,128)(2,1)S(1)}, f32[8192,128]{1,0:T(8,128)S(1)}, bf16[3,512,128]{2,1,0:T(8,128)(2,1)S(1)}) custom-call(bf16[4,512,512]{2,1,0:T(8,128)(2,1)} %x_ref.1, f32[8192,128]{1,0:T(8,128)} %bitcast.15, bf16[16,512,256]{2,1,0:T(8,128)(2,1)} %wg_hbm.1, bf16[16,512,256]{2,1,0:T(8,128)(2,1)} %wu_hbm.1, ...), custom_call_target="tpu_custom_call" | custom-call | tf_op jit(solution)/shard_map/pallas_call | solution.py:609
  75.1 2.8 %shard_map.230 = (bf16[4,512,512]{2,1,0:T(8,128)(2,1)}, f32[8192,128]{1,0:T(8,128)}, bf16[3,512,128]{2,1,0:T(8,128)(2,1)}) custom-call(bf16[4,512,512]{2,1,0:T(8,128)(2,1)S(1)} %get-tuple-element.9.y_in, f32[8192,128]{1,0:T(8,128)S(1)} %get-tuple-element.10.h_in, bf16[3,512,128]{2,1,0:T(8,128)(2,1)S(1)} %get-tuple-element.11.conv_in), custom_call_target="tpu_custom_call" | custom-call | tf_op jit(solution)/shard_map/pallas_call | solution.py:625

commit v9 on v8

--- a/solution.py
+++ b/solution.py
@@ -435,15 +435,21 @@
         for g in range(experts // GROUP - 1):
             stage_experts(t, g, *now)
             if g == 0:
-                pl.when((t >= 1) & (2 * t + 2 < chunks))(lambda: ag_relay(yg_block(2 * t + 2), 2 * t + 2))
-                pl.when((t >= 1) & (t + 1 < chunks))(lambda: ag_far(yg_block(t + 1), t + 1))
-                when_chunk(t - 4, y_three)
+                if t >= 1 and 2 * t + 2 < chunks:
+                    ag_relay(yg_block(2 * t + 2), 2 * t + 2)
+                if t >= 1 and t + 1 < chunks:
+                    ag_far(yg_block(t + 1), t + 1)
+                if t >= 4:
+                    y_three(t - 4)
             elif g == 1:
-                pl.when(t == 0)(lambda: ag_far(yg_block(1), 1))
-                pl.when(2 * t + 3 < chunks)(lambda: ag_relay(yg_block(2 * t + 3), 2 * t + 3))
-                when_chunk(t - 1, y_one)
-            else:
-                when_chunk(t - 2, y_two)
+                if t == 0:
+                    ag_far(yg_block(1), 1)
+                if 2 * t + 3 < chunks:
+                    ag_relay(yg_block(2 * t + 3), 2 * t + 3)
+                if t >= 1:
+                    y_one(t - 1)
+            elif t >= 2:
+                y_two(t - 2)
         if later is not None:
             got_yg(t + 1)
         stage_experts(t, experts // GROUP - 1, *now, mid_parts(t + 1, *later) if later is not None else ())
@@ -451,16 +457,12 @@
 
     even, odd = (m_a, prob_a), (m_b, prob_b)
 
-    def moe_body(i):
-        moe_tick(2 * i, even, odd)
-        moe_tick(2 * i + 1, odd, even)
-
     got_yg(0)
     for part in mid_parts(0, *even):
         part()
-    loop(chunks // 2 - 1, moe_body)
-    moe_tick(chunks - 2, even, odd)
-    moe_tick(chunks - 1, odd, None)
+    for t in range(chunks):
+        now, later = (even, odd) if t % 2 == 0 else (odd, even)
+        pl.when(core >= 0)(functools.partial(moe_tick, t, now, later if t + 1 < chunks else None))
     last = chunks - 1
     quarter = tokens // 4
     pieces = 2

time: 78.1 us -> 78 us (level)
  no operation moved by 1% of the time
where the time goes in v9:
time: 78 us; the launch traced here: 77.9 us
  Pallas kernels  77 us (99%)
  between operations  0.87 us (1%)
    pallas_call x1, Pallas kernels, layer_steps(): pl.pallas_call(layer_kernel, out_shape=(pltpu.VMEM(x_steps.shape, BF16),...  74.2 us
    pallas_call x1, Pallas kernels, layer_steps(): pl.pallas_call(store_kernel, out_shape=[jax.ShapeDtypeStruct(v.shape, v.d...  2.79 us

profile of v9, /device:TPU:113, one launch (start us, length us, event | category | flops | bytes accessed | tf_op | source)
XLA Modules:
  0.0 77.9 jit_solution(5290182661142934272)
XLA Ops:
  0.6 74.2 %shard_map.229 = (bf16[4,512,512]{2,1,0:T(8,128)(2,1)S(1)}, f32[8192,128]{1,0:T(8,128)S(1)}, bf16[3,512,128]{2,1,0:T(8,128)(2,1)S(1)}) custom-call(bf16[4,512,512]{2,1,0:T(8,128)(2,1)} %x_ref.1, f32[8192,128]{1,0:T(8,128)} %bitcast.15, bf16[16,512,256]{2,1,0:T(8,128)(2,1)} %wg_hbm.1, bf16[16,512,256]{2,1,0:T(8,128)(2,1)} %wu_hbm.1, ...), custom_call_target="tpu_custom_call" | custom-call | tf_op jit(solution)/shard_map/pallas_call | solution.py:611
  74.9 2.8 %shard_map.230 = (bf16[4,512,512]{2,1,0:T(8,128)(2,1)}, f32[8192,128]{1,0:T(8,128)}, bf16[3,512,128]{2,1,0:T(8,128)(2,1)}) custom-call(bf16[4,512,512]{2,1,0:T(8,128)(2,1)S(1)} %get-tuple-element.9.y_in, f32[8192,128]{1,0:T(8,128)S(1)} %get-tuple-element.10.h_in, bf16[3,512,128]{2,1,0:T(8,128)(2,1)S(1)} %get-tuple-element.11.conv_in), custom_call_target="tpu_custom_call" | custom-call | tf_op jit(solution)/shard_map/pallas_call | solution.py:627

commit v10 on v9

--- a/solution.py
+++ b/solution.py
@@ -439,8 +439,8 @@
                     ag_relay(yg_block(2 * t + 2), 2 * t + 2)
                 if t >= 1 and t + 1 < chunks:
                     ag_far(yg_block(t + 1), t + 1)
-                if t >= 4:
-                    y_three(t - 4)
+                if t >= 3:
+                    y_two(t - 3)
             elif g == 1:
                 if t == 0:
                     ag_far(yg_block(1), 1)
@@ -448,8 +448,10 @@
                     ag_relay(yg_block(2 * t + 3), 2 * t + 3)
                 if t >= 1:
                     y_one(t - 1)
-            elif t >= 2:
-                y_two(t - 2)
+                if t == chunks - 1:
+                    y_two(t - 2)
+            elif t >= 4:
+                y_three(t - 4)
         if later is not None:
             got_yg(t + 1)
         stage_experts(t, experts // GROUP - 1, *now, mid_parts(t + 1, *later) if later is not None else ())

time: 78 us -> 78.6 us (level)
  no operation moved by 1% of the time
where the time goes in v10:
time: 78.6 us; the launch traced here: 78.5 us
  Pallas kernels  77.6 us (99%)
  between operations  0.87 us (1%)
    pallas_call x1, Pallas kernels, layer_steps(): pl.pallas_call(layer_kernel, out_shape=(pltpu.VMEM(x_steps.shape, BF16),...  74.8 us
    pallas_call x1, Pallas kernels, layer_steps(): pl.pallas_call(store_kernel, out_shape=[jax.ShapeDtypeStruct(v.shape, v.d...  2.79 us

profile of v10, /device:TPU:113, one launch (start us, length us, event | category | flops | bytes accessed | tf_op | source)
XLA Modules:
  0.0 78.5 jit_solution(2180160692991670806)
XLA Ops:
  0.6 74.8 %shard_map.229 = (bf16[4,512,512]{2,1,0:T(8,128)(2,1)S(1)}, f32[8192,128]{1,0:T(8,128)S(1)}, bf16[3,512,128]{2,1,0:T(8,128)(2,1)S(1)}) custom-call(bf16[4,512,512]{2,1,0:T(8,128)(2,1)} %x_ref.1, f32[8192,128]{1,0:T(8,128)} %bitcast.15, bf16[16,512,256]{2,1,0:T(8,128)(2,1)} %wg_hbm.1, bf16[16,512,256]{2,1,0:T(8,128)(2,1)} %wu_hbm.1, ...), custom_call_target="tpu_custom_call" | custom-call | tf_op jit(solution)/shard_map/pallas_call | solution.py:613
  75.5 2.8 %shard_map.230 = (bf16[4,512,512]{2,1,0:T(8,128)(2,1)}, f32[8192,128]{1,0:T(8,128)}, bf16[3,512,128]{2,1,0:T(8,128)(2,1)}) custom-call(bf16[4,512,512]{2,1,0:T(8,128)(2,1)S(1)} %get-tuple-element.9.y_in, f32[8192,128]{1,0:T(8,128)S(1)} %get-tuple-element.10.h_in, bf16[3,512,128]{2,1,0:T(8,128)(2,1)S(1)} %get-tuple-element.11.conv_in), custom_call_target="tpu_custom_call" | custom-call | tf_op jit(solution)/shard_map/pallas_call | solution.py:629
